TPU v7x, 1024 devices: a whole 4x8x16 slice. The times are simulated.
1024 devices in a mesh: face: 32 (over z_lo, y), col: 32 (over z_hi, x, core).
Axes of the slice: x: 4, y: 8, z: 16 (z_hi: 4, z_lo: 4; z = z_hi * 4 + z_lo), core: 2. Of those that a mesh axis runs over, the one named last changes fastest.
Arguments:
- fields: float32 [4, 640, 640, 128], P(None, 'face', 'col'), may hold values from -6 to 6
- metric_diag: float32 [2, 640, 640], P(None, 'face', 'col'), may hold values from 0.05 to 0.5
- metric_cross: float32 [640, 640], P('face', 'col'), may hold values from -0.1 to 0.1
- point_mass: float32 [640, 640], P('face', 'col'), may hold values from 0.5 to 2
Outputs:
- biharmonic: float32 [4, 640, 640, 128], P(None, 'face', 'col')
All inputs are finite; a program needn't handle non-finite values.
Results may differ from a plain program's by a relative error of at most 0.00024.
Values sent between devices are 32-bit elements; how exact they have to be, the bound alone decides.
A program may use at most 32 MiB of HBM per device.

v0:
```python
import jax
import jax.numpy as jnp
import numpy as np
from jax import lax
from jax.sharding import PartitionSpec as P


def with_halo(array, sides, width):
    for axis, dim in sides:
        devices, length = (lax.axis_size(axis), array.shape[dim])
        up = [(i, (i + 1) % devices) for i in range(devices)]
        down = [(j, i) for i, j in up]
        last = lax.slice_in_dim(array, length - width, length, axis=dim)
        first = lax.slice_in_dim(array, 0, width, axis=dim)
        before = lax.ppermute(last, axis, up)
        after = lax.ppermute(first, axis, down)
        array = jnp.concatenate([before, array, after], axis=dim)
    return array


def derivative_table():
    small = 1.0 / np.sqrt(5.0)
    nodes = np.array([-1.0, -small, small, 1.0])
    count = nodes.shape[0]
    weights = np.array(
        [np.prod([nodes[a] - nodes[k] for k in range(count) if k != a]) for a in range(count)]
    )
    table = np.zeros((count, count))
    for a in range(count):
        for b in range(count):
            if a == b:
                table[a, b] = np.sum([1.0 / (nodes[a] - nodes[k]) for k in range(count) if k != a])
            else:
                table[a, b] = weights[a] / weights[b] / (nodes[a] - nodes[b])
    return jnp.asarray(table, jnp.float32)


def laplace(values, metric_diag, metric_cross):
    table = derivative_table()
    nfield, rows, cols, nlev = values.shape
    blocks_x = rows // 4
    blocks_y = cols // 4
    shaped = values.reshape(nfield, blocks_x, 4, blocks_y, 4, nlev)
    first_diag = metric_diag[0].reshape(1, blocks_x, 4, blocks_y, 4, 1)
    second_diag = metric_diag[1].reshape(1, blocks_x, 4, blocks_y, 4, 1)
    cross_term = metric_cross.reshape(1, blocks_x, 4, blocks_y, 4, 1)
    high = lax.Precision.HIGHEST
    grad_x = jnp.einsum("ab,febgcl->feagcl", table, shaped, precision=high)
    grad_y = jnp.einsum("cd,febgdl->febgcl", table, shaped, precision=high)
    flux_x = first_diag * grad_x + cross_term * grad_y
    flux_y = cross_term * grad_x + second_diag * grad_y
    weak = jnp.einsum("ba,febgcl->feagcl", table, flux_x, precision=high)
    weak = weak + jnp.einsum("dc,febgdl->febgcl", table, flux_y, precision=high)
    return (-weak).reshape(nfield, rows, cols, nlev)


def assemble(padded):
    rows = padded.shape[1] - 2
    cols = padded.shape[2] - 2
    row_local = jnp.arange(rows, dtype=jnp.int32) % 4
    col_local = jnp.arange(cols, dtype=jnp.int32) % 4
    row_low = (row_local == 0).astype(jnp.float32).reshape(1, rows, 1, 1)
    row_high = (row_local == 3).astype(jnp.float32).reshape(1, rows, 1, 1)
    col_low = (col_local == 0).astype(jnp.float32).reshape(1, 1, cols, 1)
    col_high = (col_local == 3).astype(jnp.float32).reshape(1, 1, cols, 1)
    summed = padded[:, 1:-1] + row_low * padded[:, :-2] + row_high * padded[:, 2:]
    return summed[:, :, 1:-1] + col_low * summed[:, :, :-2] + col_high * summed[:, :, 2:]


def shards(fields, metric_diag, metric_cross, point_mass):
    local_mass = point_mass[None, :, :, None]
    first_lap = laplace(fields, metric_diag, metric_cross)
    padded_lap, padded_mass = (
        with_halo(first_lap, (("face", 1), ("col", 2)), 1),
        with_halo(local_mass, (("face", 1), ("col", 2)), 1),
    )
    mass_sum = assemble(padded_mass)
    first = assemble(padded_lap) / mass_sum
    second_lap = laplace(first, metric_diag, metric_cross)
    padded_second = with_halo(second_lap, (("face", 1), ("col", 2)), 1)
    return assemble(padded_second) / mass_sum


def solution(mesh):
    return jax.shard_map(
        shards,
        mesh=mesh,
        in_specs=(
            P(None, "face", "col", None),
            P(None, "face", "col"),
            P("face", "col"),
            P("face", "col"),
        ),
        out_specs=P(None, "face", "col", None),
        check_vma=False,
    )
```

profile of v0, /device:TPU:7, one launch (start us, length us, event | category | flops | bytes accessed | tf_op | source)
XLA Modules:
  0.0 104.6 jit_solution(10204850547475052714)
XLA Ops:
  0.0 0.0 copy-start
  0.0 0.8 fusion.41
  0.8 3.2 %collective-permute-start.4 = (f32[1,1,20,1]{2,1,3,0:T(1,128)S(1)}, f32[1,1,20,1]{2,1,3,0:T(1,128)S(1)}, u32[]{:S(2)}, u32[]{:S(2)}) collective-permute-start(f32[1,1,20,1]{2,1,3,0:T(1,128)S(1)} %get-tuple-element.17), channel_id=1, source_target_pairs={{0,32},{32,64},{64,96},{96,128},{128,160},{160,192},{192,224},{224... | collective-permute-start | bytes 248 | tf_op jit(solution)/shard_map/ppermute | solution.py:15
  4.0 9.2 %collective-permute-start.5 = (f32[1,1,20,1]{2,1,3,0:T(1,128)S(1)}, f32[1,1,20,1]{2,1,3,0:T(1,128)S(1)}, u32[]{:S(2)}, u32[]{:S(2)}) collective-permute-start(f32[1,1,20,1]{2,1,3,0:T(1,128)S(1)} %get-tuple-element.18), channel_id=1, source_target_pairs={{32,0},{64,32},{96,64},{128,96},{160,128},{192,160},{224,192},{256... | collective-permute-start | bytes 248 | tf_op jit(solution)/shard_map/ppermute | solution.py:16
  13.2 0.9 slice_reduce_fusion.1
  14.1 0.1 mul.170
  14.2 0.3 copy.26
  14.4 0.1 mul.179
  14.5 0.0 copy-start.3
  14.5 0.3 copy.33
  14.8 0.4 copy-done.3
  15.2 0.1 mul.173
  15.3 0.0 copy-start.1
  15.3 0.3 copy.28
  15.6 0.0 copy-done
  15.6 0.4 copy-done.1
  16.0 1.5 %fusion.21 = f32[4,4,5,4,5,128]{5,0,4,3,2,1:T(4,128)S(1)} fusion(f32[4,4,1,1,1,1]{1,0,5,4,3,2:T(4,128)S(1)} %copy-done.1, f32[4,5,4,5,4,128]{5,0,4,3,2,1:T(4,128)S(1)} %bitcast.61), kind=kOutput, calls=%fused_computation.41 | convolution fusion | flops 9830400 | bytes 1638464 | tf_op jit(solution)/shard_map/cd,febgdl->febgcl/dot_general | solution.py:49
  17.5 2.0 %bitcast_add_fusion.3 = (f32[4,5,4,5,4,128]{5,2,4,3,1,0:T(4,128)S(1)}, f32[4,5,4,5,4,128]{5,2,4,3,1,0:T(4,128)S(1)}) fusion(f32[4,4,5,4,5,128]{5,0,4,3,2,1:T(4,128)S(1)} %fusion.21, f32[5,4,5,4]{1,3,2,0:T(4,128)S(1)} %copy.33, f32[5,4,5,4]{1,3,2,0:T(4,128)S(1)} %copy.28, f32[4,4,1,1,1,1]{1,0,5,4,3,2:T(4,128)S(1)} %copy-done.1, ...), kind=kOutput, calls=%fused_computation.30 | convolution fusion | flops 10444800 | bytes 3280064 | tf_op jit(solution)/shard_map/ab,febgcl->feagcl/dot_general | solution.py:48
  19.5 1.6 %fusion.19 = f32[4,5,4,5,128,4]{4,5,3,2,1,0:T(4,128)S(1)} fusion(f32[4,4,1,1,1,1]{1,0,5,4,3,2:T(4,128)S(1)} %copy-done.1, f32[4,5,4,5,4,128]{5,2,4,3,1,0:T(4,128)S(1)} %get-tuple-element.19), kind=kOutput, calls=%fused_computation.39 | convolution fusion | flops 9830400 | bytes 1638464 | tf_op jit(solution)/shard_map/dc,febgdl->febgcl/dot_general | solution.py:53
  21.0 1.9 %fusion.1 = f32[4,5,4,5,4,128]{5,2,4,3,1,0:T(4,128)S(1)} fusion(f32[4,4,1,1,1,1]{1,0,5,4,3,2:T(4,128)S(1)} %copy-done.1, f32[4,5,4,5,128,4]{4,5,3,2,1,0:T(4,128)S(1)} %fusion.19, f32[4,5,4,5,4,128]{5,2,4,3,1,0:T(4,128)S(1)} %get-tuple-element.20, f32[4,4,5,4,5,128]{5,0,4,3,2,1:T(4,128)S(1)} %fusion.21, f32[5,4,5,4]{1,3,2,0:T(4,128)S(1)} %copy.28, ...), kind=kOutput, calls=%fused_computation.5 | convolution fusion | flops 10854400 | bytes 3280064 | tf_op jit(solution)/shard_map/ba,febgcl->feagcl/dot_general | solution.py:52
  23.0 0.3 copy.37
  23.3 0.0 copy-start.2
  23.3 1.9 %collective-permute-start = (f32[4,1,20,128]{3,0,2,1:T(4,128)S(1)}, f32[4,1,20,128]{3,0,2,1:T(4,128)S(1)}, u32[]{:S(2)}, u32[]{:S(2)}) collective-permute-start(f32[4,1,20,128]{3,0,2,1:T(4,128)S(1)} %get-tuple-element.13), channel_id=1, source_target_pairs={{0,32},{32,64},{64,96},{96,128},{128,160},{160,192},{192,224},{224... | collective-permute-start | bytes 122888 | tf_op jit(solution)/shard_map/ppermute | solution.py:15
  25.3 7.3 %collective-permute-start.1 = (f32[4,1,20,128]{3,0,2,1:T(4,128)S(1)}, f32[4,1,20,128]{3,0,2,1:T(4,128)S(1)}, u32[]{:S(2)}, u32[]{:S(2)}) collective-permute-start(f32[4,1,20,128]{3,0,2,1:T(4,128)S(1)} %get-tuple-element.14), channel_id=1, source_target_pairs={{32,0},{64,32},{96,64},{128,96},{160,128},{192,160},{224,192},{256... | collective-permute-start | bytes 122888 | tf_op jit(solution)/shard_map/ppermute | solution.py:16
  32.5 0.0 collective-permute-done.4
  32.6 0.0 collective-permute-done.5
  32.6 0.0 copy-done.2
  32.6 0.1 fusion.40
  32.7 11.9 %collective-permute-start.6 = (f32[1,22,1,1]{2,1,3,0:T(8,128)S(1)}, f32[1,22,1,1]{2,1,3,0:T(8,128)S(1)}, u32[]{:S(2)}, u32[]{:S(2)}) collective-permute-start(f32[1,22,1,1]{2,1,3,0:T(8,128)S(1)} %get-tuple-element.15), channel_id=1, source_target_pairs={{0,1},{1,2},{2,3},{3,4},{4,5},{5,6},{6,7},{7,8},{8,9},{9,10},{10,1... | collective-permute-start | bytes 272 | tf_op jit(solution)/shard_map/ppermute | solution.py:15
  44.6 1.9 %collective-permute-start.7 = (f32[1,22,1,1]{2,1,3,0:T(8,128)S(1)}, f32[1,22,1,1]{2,1,3,0:T(8,128)S(1)}, u32[]{:S(2)}, u32[]{:S(2)}) collective-permute-start(f32[1,22,1,1]{2,1,3,0:T(8,128)S(1)} %get-tuple-element.16), channel_id=1, source_target_pairs={{1,0},{2,1},{3,2},{4,3},{5,4},{6,5},{7,6},{8,7},{9,8},{10,9},{11,1... | collective-permute-start | bytes 272 | tf_op jit(solution)/shard_map/ppermute | solution.py:16
  46.5 0.0 collective-permute-done.6
  46.6 9.1 %collective-permute-done.7 = f32[1,22,1,1]{2,1,3,0:T(8,128)S(1)} collective-permute-done((f32[1,22,1,1]{2,1,3,0:T(8,128)S(1)}, f32[1,22,1,1]{2,1,3,0:T(8,128)S(1)}, u32[]{:S(2)}, u32[]{:S(2)}) %collective-permute-start.7) | collective-permute-done | bytes 120 | tf_op jit(solution)/shard_map/ppermute | solution.py:16
  55.6 0.1 pad_maximum_fusion.9
  55.7 0.1 fusion.36
  55.8 0.0 collective-permute-done
  55.8 0.0 collective-permute-done.1
  55.9 1.9 %collective-permute-start.2 = (f32[4,22,1,128]{3,0,2,1:T(4,128)S(1)}, f32[4,22,1,128]{3,0,2,1:T(4,128)S(1)}, u32[]{:S(2)}, u32[]{:S(2)}) collective-permute-start(f32[4,22,1,128]{3,0,2,1:T(4,128)S(1)} %get-tuple-element.9), channel_id=1, source_target_pairs={{0,1},{1,2},{2,3},{3,4},{4,5},{5,6},{6,7},{7,8},{8,9},{9,10},{10,1... | collective-permute-start | bytes 135176 | tf_op jit(solution)/shard_map/ppermute | solution.py:15
  57.8 2.6 %collective-permute-start.3 = (f32[4,22,1,128]{3,0,2,1:T(4,128)S(1)}, f32[4,22,1,128]{3,0,2,1:T(4,128)S(1)}, u32[]{:S(2)}, u32[]{:S(2)}) collective-permute-start(f32[4,22,1,128]{3,0,2,1:T(4,128)S(1)} %get-tuple-element.10), channel_id=1, source_target_pairs={{1,0},{2,1},{3,2},{4,3},{5,4},{6,5},{7,6},{8,7},{9,8},{10,9},{11,1... | collective-permute-start | bytes 135176 | tf_op jit(solution)/shard_map/ppermute | solution.py:16
  60.4 0.1 fusion.34
  60.5 0.0 collective-permute-done.2
  60.5 8.7 %collective-permute-done.3 = f32[4,22,1,128]{3,0,2,1:T(4,128)S(1)} collective-permute-done((f32[4,22,1,128]{3,0,2,1:T(4,128)S(1)}, f32[4,22,1,128]{3,0,2,1:T(4,128)S(1)}, u32[]{:S(2)}, u32[]{:S(2)}) %collective-permute-start.3) | collective-permute-done | bytes 45088 | tf_op jit(solution)/shard_map/ppermute | solution.py:16
  69.2 0.2 pad_maximum_fusion
  69.4 0.3 fusion.6
  69.7 0.7 fusion.12
  70.5 1.5 %fusion.16 = f32[4,5,4,5,128,4]{4,5,3,2,1,0:T(4,128)S(1)} fusion(f32[4,4,1,1,1,1]{1,0,5,4,3,2:T(4,128)S(1)} %copy-done.1, f32[4,5,4,5,4,128]{5,0,4,3,2,1:T(4,128)S(1)} %bitcast.68), kind=kOutput, calls=%fused_computation.36 | convolution fusion | flops 9830400 | bytes 1638464 | tf_op jit(solution)/shard_map/cd,febgdl->febgcl/dot_general | solution.py:49
  72.0 2.0 %bitcast_add_fusion = (f32[4,5,4,5,4,128]{5,2,4,3,1,0:T(4,128)S(1)}, f32[4,5,4,5,4,128]{5,2,4,3,1,0:T(4,128)S(1)}) fusion(f32[4,5,4,5,128,4]{4,5,3,2,1,0:T(4,128)S(1)} %fusion.16, f32[5,4,5,4]{1,3,2,0:T(4,128)S(1)} %copy.33, f32[5,4,5,4]{1,3,2,0:T(4,128)S(1)} %copy.28, f32[4,4,1,1,1,1]{1,0,5,4,3,2:T(4,128)S(1)} %copy-done.1, ...), kind=kOutput, calls=%fused_computation.28 | convolution fusion | flops 10444800 | bytes 3280064 | tf_op jit(solution)/shard_map/ab,febgcl->feagcl/dot_general | solution.py:48
  74.0 1.6 %fusion.14 = f32[4,5,4,5,128,4]{4,5,3,2,1,0:T(4,128)S(1)} fusion(f32[4,4,1,1,1,1]{1,0,5,4,3,2:T(4,128)S(1)} %copy-done.1, f32[4,5,4,5,4,128]{5,2,4,3,1,0:T(4,128)S(1)} %get-tuple-element.21), kind=kOutput, calls=%fused_computation.34 | convolution fusion | flops 9830400 | bytes 1638464 | tf_op jit(solution)/shard_map/dc,febgdl->febgcl/dot_general | solution.py:53
  75.6 1.9 %fusion.3 = f32[4,5,4,5,4,128]{5,2,4,3,1,0:T(4,128)S(1)} fusion(f32[4,4,1,1,1,1]{1,0,5,4,3,2:T(4,128)S(1)} %copy-done.1, f32[4,5,4,5,128,4]{4,5,3,2,1,0:T(4,128)S(1)} %fusion.14, f32[4,5,4,5,4,128]{5,2,4,3,1,0:T(4,128)S(1)} %get-tuple-element.22, f32[4,5,4,5,128,4]{4,5,3,2,1,0:T(4,128)S(1)} %fusion.16, f32[5,4,5,4]{1,3,2,0:T(4,128)S(1)} %copy.28, ...), kind=kOutput, calls=%fused_computation.7 | convolution fusion | flops 10854400 | bytes 3280064 | tf_op jit(solution)/shard_map/ba,febgcl->feagcl/dot_general | solution.py:52
  77.5 0.3 copy.46
  77.9 1.9 %collective-permute-start.8 = (f32[4,1,20,128]{3,0,2,1:T(4,128)S(1)}, f32[4,1,20,128]{3,0,2,1:T(4,128)S(1)}, u32[]{:S(2)}, u32[]{:S(2)}) collective-permute-start(f32[4,1,20,128]{3,0,2,1:T(4,128)S(1)} %get-tuple-element.11), channel_id=1, source_target_pairs={{0,32},{32,64},{64,96},{96,128},{128,160},{160,192},{192,224},{224... | collective-permute-start | bytes 122888 | tf_op jit(solution)/shard_map/ppermute | solution.py:15
  79.8 7.3 %collective-permute-start.9 = (f32[4,1,20,128]{3,0,2,1:T(4,128)S(1)}, f32[4,1,20,128]{3,0,2,1:T(4,128)S(1)}, u32[]{:S(2)}, u32[]{:S(2)}) collective-permute-start(f32[4,1,20,128]{3,0,2,1:T(4,128)S(1)} %get-tuple-element.12), channel_id=1, source_target_pairs={{32,0},{64,32},{96,64},{128,96},{160,128},{192,160},{224,192},{256... | collective-permute-start | bytes 122888 | tf_op jit(solution)/shard_map/ppermute | solution.py:16
  87.1 0.0 collective-permute-done.8
  87.1 1.1 %collective-permute-done.9 = f32[4,1,20,128]{3,0,2,1:T(4,128)S(1)} collective-permute-done((f32[4,1,20,128]{3,0,2,1:T(4,128)S(1)}, f32[4,1,20,128]{3,0,2,1:T(4,128)S(1)}, u32[]{:S(2)}, u32[]{:S(2)}) %collective-permute-start.9) | collective-permute-done | bytes 40992 | tf_op jit(solution)/shard_map/ppermute | solution.py:16
  88.2 3.0 %collective-permute-start.10 = (f32[4,22,1,128]{3,0,2,1:T(4,128)S(1)}, f32[4,22,1,128]{3,0,2,1:T(4,128)S(1)}, u32[]{:S(2)}, u32[]{:S(2)}) collective-permute-start(f32[4,22,1,128]{3,0,2,1:T(4,128)S(1)} %get-tuple-element.7), channel_id=1, source_target_pairs={{0,1},{1,2},{2,3},{3,4},{4,5},{5,6},{6,7},{7,8},{8,9},{9,10},{10,1... | collective-permute-start | bytes 135176 | tf_op jit(solution)/shard_map/ppermute | solution.py:15
  91.2 1.9 %collective-permute-start.11 = (f32[4,22,1,128]{3,0,2,1:T(4,128)S(1)}, f32[4,22,1,128]{3,0,2,1:T(4,128)S(1)}, u32[]{:S(2)}, u32[]{:S(2)}) collective-permute-start(f32[4,22,1,128]{3,0,2,1:T(4,128)S(1)} %get-tuple-element.8), channel_id=1, source_target_pairs={{1,0},{2,1},{3,2},{4,3},{5,4},{6,5},{7,6},{8,7},{9,8},{10,9},{11,1... | collective-permute-start | bytes 135176 | tf_op jit(solution)/shard_map/ppermute | solution.py:16
  93.1 0.0 collective-permute-done.10
  93.2 9.4 %collective-permute-done.11 = f32[4,22,1,128]{3,0,2,1:T(4,128)S(1)} collective-permute-done((f32[4,22,1,128]{3,0,2,1:T(4,128)S(1)}, f32[4,22,1,128]{3,0,2,1:T(4,128)S(1)}, u32[]{:S(2)}, u32[]{:S(2)}) %collective-permute-start.11) | collective-permute-done | bytes 45088 | tf_op jit(solution)/shard_map/ppermute | solution.py:16
  102.6 0.2 pad_maximum_fusion.1
  102.8 0.3 fusion.4
  103.2 1.5 %fusion.9 = f32[4,20,20,128]{3,0,2,1:T(4,128)} fusion(f32[4,20,22,128]{3,0,2,1:T(4,128)S(1)} %fusion.4, f32[20,20]{1,0:T(8,128)S(1)} %fusion.34, f32[20]{0:T(128)S(1)} %get-tuple-element.23, f32[20]{0:T(128)S(1)} %get-tuple-element.24), kind=kLoop, calls=%fused_computation.20 | loop fusion | flops 1024000 | bytes 3278560 | tf_op jit(solution)/shard_map/div | solution.py:81
  (6 shorter events, 0.1 us)
Async XLA Ops:
  0.0 15.6 %copy-start = (f32[4,20,20,128]{3,0,2,1:T(4,128)S(1)}, f32[4,20,20,128]{3,0,2,1:T(4,128)}, u32[]{:S(2)}) copy-start(f32[4,20,20,128]{3,0,2,1:T(4,128)} %param.6) | copy-start | bytes 2457604
  0.8 31.8 %collective-permute-start.4 = (f32[1,1,20,1]{2,1,3,0:T(1,128)S(1)}, f32[1,1,20,1]{2,1,3,0:T(1,128)S(1)}, u32[]{:S(2)}, u32[]{:S(2)}) collective-permute-start(f32[1,1,20,1]{2,1,3,0:T(1,128)S(1)} %get-tuple-element.17), channel_id=1, source_target_pairs={{0,32},{32,64},{64,96},{96,128},{128,160},{160,192},{192,224},{224... | collective-permute-start | bytes 248 | tf_op jit(solution)/shard_map/ppermute | solution.py:15
  4.0 28.6 %collective-permute-start.5 = (f32[1,1,20,1]{2,1,3,0:T(1,128)S(1)}, f32[1,1,20,1]{2,1,3,0:T(1,128)S(1)}, u32[]{:S(2)}, u32[]{:S(2)}) collective-permute-start(f32[1,1,20,1]{2,1,3,0:T(1,128)S(1)} %get-tuple-element.18), channel_id=1, source_target_pairs={{32,0},{64,32},{96,64},{128,96},{160,128},{192,160},{224,192},{256... | collective-permute-start | bytes 248 | tf_op jit(solution)/shard_map/ppermute | solution.py:16
  14.5 0.7 copy-start.3
  15.3 0.7 copy-start.1
  23.3 9.3 %copy-start.2 = (f32[20,20]{1,0:T(8,128)S(1)}, f32[20,20]{1,0:T(8,128)}, u32[]{:S(2)}) copy-start(f32[20,20]{1,0:T(8,128)} %param.9) | copy-start | bytes 4804
  23.3 32.5 %collective-permute-start = (f32[4,1,20,128]{3,0,2,1:T(4,128)S(1)}, f32[4,1,20,128]{3,0,2,1:T(4,128)S(1)}, u32[]{:S(2)}, u32[]{:S(2)}) collective-permute-start(f32[4,1,20,128]{3,0,2,1:T(4,128)S(1)} %get-tuple-element.13), channel_id=1, source_target_pairs={{0,32},{32,64},{64,96},{96,128},{128,160},{160,192},{192,224},{224... | collective-permute-start | bytes 122888 | tf_op jit(solution)/shard_map/ppermute | solution.py:15
  25.3 30.6 %collective-permute-start.1 = (f32[4,1,20,128]{3,0,2,1:T(4,128)S(1)}, f32[4,1,20,128]{3,0,2,1:T(4,128)S(1)}, u32[]{:S(2)}, u32[]{:S(2)}) collective-permute-start(f32[4,1,20,128]{3,0,2,1:T(4,128)S(1)} %get-tuple-element.14), channel_id=1, source_target_pairs={{32,0},{64,32},{96,64},{128,96},{160,128},{192,160},{224,192},{256... | collective-permute-start | bytes 122888 | tf_op jit(solution)/shard_map/ppermute | solution.py:16
  32.7 13.9 %collective-permute-start.6 = (f32[1,22,1,1]{2,1,3,0:T(8,128)S(1)}, f32[1,22,1,1]{2,1,3,0:T(8,128)S(1)}, u32[]{:S(2)}, u32[]{:S(2)}) collective-permute-start(f32[1,22,1,1]{2,1,3,0:T(8,128)S(1)} %get-tuple-element.15), channel_id=1, source_target_pairs={{0,1},{1,2},{2,3},{3,4},{4,5},{5,6},{6,7},{7,8},{8,9},{9,10},{10,1... | collective-permute-start | bytes 272 | tf_op jit(solution)/shard_map/ppermute | solution.py:15
  44.6 11.0 %collective-permute-start.7 = (f32[1,22,1,1]{2,1,3,0:T(8,128)S(1)}, f32[1,22,1,1]{2,1,3,0:T(8,128)S(1)}, u32[]{:S(2)}, u32[]{:S(2)}) collective-permute-start(f32[1,22,1,1]{2,1,3,0:T(8,128)S(1)} %get-tuple-element.16), channel_id=1, source_target_pairs={{1,0},{2,1},{3,2},{4,3},{5,4},{6,5},{7,6},{8,7},{9,8},{10,9},{11,1... | collective-permute-start | bytes 272 | tf_op jit(solution)/shard_map/ppermute | solution.py:16
  55.9 4.6 %collective-permute-start.2 = (f32[4,22,1,128]{3,0,2,1:T(4,128)S(1)}, f32[4,22,1,128]{3,0,2,1:T(4,128)S(1)}, u32[]{:S(2)}, u32[]{:S(2)}) collective-permute-start(f32[4,22,1,128]{3,0,2,1:T(4,128)S(1)} %get-tuple-element.9), channel_id=1, source_target_pairs={{0,1},{1,2},{2,3},{3,4},{4,5},{5,6},{6,7},{7,8},{8,9},{9,10},{10,1... | collective-permute-start | bytes 135176 | tf_op jit(solution)/shard_map/ppermute | solution.py:15
  57.8 11.4 %collective-permute-start.3 = (f32[4,22,1,128]{3,0,2,1:T(4,128)S(1)}, f32[4,22,1,128]{3,0,2,1:T(4,128)S(1)}, u32[]{:S(2)}, u32[]{:S(2)}) collective-permute-start(f32[4,22,1,128]{3,0,2,1:T(4,128)S(1)} %get-tuple-element.10), channel_id=1, source_target_pairs={{1,0},{2,1},{3,2},{4,3},{5,4},{6,5},{7,6},{8,7},{9,8},{10,9},{11,1... | collective-permute-start | bytes 135176 | tf_op jit(solution)/shard_map/ppermute | solution.py:16
  77.9 9.2 %collective-permute-start.8 = (f32[4,1,20,128]{3,0,2,1:T(4,128)S(1)}, f32[4,1,20,128]{3,0,2,1:T(4,128)S(1)}, u32[]{:S(2)}, u32[]{:S(2)}) collective-permute-start(f32[4,1,20,128]{3,0,2,1:T(4,128)S(1)} %get-tuple-element.11), channel_id=1, source_target_pairs={{0,32},{32,64},{64,96},{96,128},{128,160},{160,192},{192,224},{224... | collective-permute-start | bytes 122888 | tf_op jit(solution)/shard_map/ppermute | solution.py:15
  79.8 8.4 %collective-permute-start.9 = (f32[4,1,20,128]{3,0,2,1:T(4,128)S(1)}, f32[4,1,20,128]{3,0,2,1:T(4,128)S(1)}, u32[]{:S(2)}, u32[]{:S(2)}) collective-permute-start(f32[4,1,20,128]{3,0,2,1:T(4,128)S(1)} %get-tuple-element.12), channel_id=1, source_target_pairs={{32,0},{64,32},{96,64},{128,96},{160,128},{192,160},{224,192},{256... | collective-permute-start | bytes 122888 | tf_op jit(solution)/shard_map/ppermute | solution.py:16
  88.2 5.0 %collective-permute-start.10 = (f32[4,22,1,128]{3,0,2,1:T(4,128)S(1)}, f32[4,22,1,128]{3,0,2,1:T(4,128)S(1)}, u32[]{:S(2)}, u32[]{:S(2)}) collective-permute-start(f32[4,22,1,128]{3,0,2,1:T(4,128)S(1)} %get-tuple-element.7), channel_id=1, source_target_pairs={{0,1},{1,2},{2,3},{3,4},{4,5},{5,6},{6,7},{7,8},{8,9},{9,10},{10,1... | collective-permute-start | bytes 135176 | tf_op jit(solution)/shard_map/ppermute | solution.py:15
  91.2 11.4 %collective-permute-start.11 = (f32[4,22,1,128]{3,0,2,1:T(4,128)S(1)}, f32[4,22,1,128]{3,0,2,1:T(4,128)S(1)}, u32[]{:S(2)}, u32[]{:S(2)}) collective-permute-start(f32[4,22,1,128]{3,0,2,1:T(4,128)S(1)} %get-tuple-element.8), channel_id=1, source_target_pairs={{1,0},{2,1},{3,2},{4,3},{5,4},{6,5},{7,6},{8,7},{9,8},{10,9},{11,1... | collective-permute-start | bytes 135176 | tf_op jit(solution)/shard_map/ppermute | solution.py:16
where the time goes:
time: 105 us
  starting transfers between devices  54.1 us (52%)
  waiting for transfers between devices  28.4 us (27%)
  matrix products  14 us (13%)
  local copies, waits for them, and re-layouts  4.25 us (4%)
  other arithmetic  3.6 us (3%)
    ppermute x6, starting transfers between devices, with_halo(): after = lax.ppermute(first, axis, down)  30.2 us
    ppermute x6, waiting for transfers between devices, with_halo(): after = lax.ppermute(first, axis, down)  28.3 us
    ppermute x6, starting transfers between devices, with_halo(): before = lax.ppermute(last, axis, up)  23.9 us
    dot_general x2, matrix products, laplace(): grad_x = jnp.einsum('ab,febgcl->feagcl', table, shaped, precision=high)  3.99 us
    dot_general x2, matrix products, laplace(): weak = jnp.einsum('ba,febgcl->feagcl', table, flux_x, precision=high)  3.87 us
    dot_general x2, matrix products, laplace(): weak = weak + jnp.einsum('dc,febgdl->febgcl', table, flux_y, precision=high)  3.1 us
    dot_general x2, matrix products, laplace(): grad_y = jnp.einsum('cd,febgdl->febgcl', table, shaped, precision=high)  2.99 us
  transfers between devices with their start and end apart: 12, of which 4 were waited for; matrix products, arithmetic and copies ran while one was open for 9% of the time, Pallas kernels for 0%

commit v1 on v0

v1 whole, which is shorter than its diff:
```python
import functools

import jax
import jax.numpy as jnp
import numpy as np
from jax import lax
from jax.experimental import pallas as pl
from jax.experimental.pallas import tpu as pltpu
from jax.sharding import PartitionSpec as P

MESH = pl.DeviceIdType.MESH
SUB = 8
LANES = 128


def derivative_table():
    small = 1.0 / np.sqrt(5.0)
    nodes = np.array([-1.0, -small, small, 1.0])
    count = nodes.shape[0]
    weights = np.array(
        [np.prod([nodes[a] - nodes[k] for k in range(count) if k != a]) for a in range(count)]
    )
    table = np.zeros((count, count))
    for a in range(count):
        for b in range(count):
            if a == b:
                table[a, b] = np.sum([1.0 / (nodes[a] - nodes[k]) for k in range(count) if k != a])
            else:
                table[a, b] = weights[a] / weights[b] / (nodes[a] - nodes[b])
    table[np.abs(table) < 1e-12] = 0.0
    return table


def combine(table, parts):
    out = []
    for a in range(4):
        total = None
        for b in range(4):
            if table[a, b] == 0.0:
                continue
            term = np.float32(table[a, b]) * parts[b]
            total = term if total is None else total + term
        out.append(total)
    return out


def shift_coefficients(table):
    local = lax.broadcasted_iota(jnp.int32, (SUB, LANES), 0) % 4
    result = {}
    for s in range(-3, 4):
        value = jnp.zeros((SUB, LANES), jnp.float32)
        for c in range(4):
            if 0 <= c + s < 4:
                value = jnp.where(local == c, np.float32(table[c, c + s]), value)
        result[s] = value
    return result


def along(tile, coefficients):
    total = coefficients[0] * tile
    for s in (-3, -2, -1, 1, 2, 3):
        total = total + coefficients[s] * pltpu.roll(tile, (-s) % SUB, 0)
    return total


def operator_kernel(
    faces, cols_axis, nfield, rows, cols,
    fields, diag, cross, mass,
    out,
    u, md, mc, mp, mpad, mrow, mside, mcorner, weights,
    lap1, lap2, send_w, send_e, halo_w, halo_e, result,
    load_sem, store_sem, mass_send, mass_recv, edge_send, edge_recv,
):
    table = derivative_table()
    blocks = rows // 4
    tiles = -(-cols // SUB)
    wide = tiles * SUB
    face = lax.axis_index("face")
    col = lax.axis_index("col")
    up, down = lax.rem(face + faces - 1, faces), lax.rem(face + 1, faces)
    left, right = lax.rem(col + cols_axis - 1, cols_axis), lax.rem(col + 1, cols_axis)
    partners = (
        (up, col), (down, col), (face, left), (face, right),
        (up, left), (up, right), (down, left), (down, right),
    )

    barrier = pltpu.get_barrier_semaphore()
    for partner in partners:
        pl.semaphore_signal(barrier, inc=1, device_id=partner, device_id_type=MESH)

    small_loads = [
        pltpu.make_async_copy(source, target, load_sem.at[nfield + k])
        for k, (source, target) in enumerate(((diag, md), (cross, mc), (mass, mp)))
    ]
    field_loads = [
        pltpu.make_async_copy(fields.at[f], u.at[f], load_sem.at[f]) for f in range(nfield)
    ]
    for load in small_loads + field_loads:
        load.start()

    sub = lax.broadcasted_iota(jnp.int32, (SUB, LANES), 0)

    def spread(k, square):
        turned = jnp.transpose(square)
        for r in range(rows):
            weights[k, r] = jnp.broadcast_to(turned[:wide, r : r + 1], (wide, LANES))

    def padded(value):
        block = jnp.zeros((LANES, LANES), jnp.float32)
        return lax.pad(value, np.float32(0), ((0, LANES - rows, 0), (0, LANES - cols, 0)))

    for load in small_loads:
        load.wait()
    mpad[...] = padded(mp[...])[:wide]
    spread(0, padded(md[0]))
    spread(1, padded(md[1]))
    spread(2, padded(mc[...]))

    forward = shift_coefficients(table)
    backward = shift_coefficients(table.T)

    def laplace(values, e, v):
        window = pl.ds(v * SUB, SUB)
        grad_x = combine(table, values)
        grad_y = [along(x, forward) for x in values]
        flux_x, flux_y = [], []
        for a in range(4):
            first, second, mixed = (weights[k, 4 * e + a, window, :] for k in range(3))
            flux_x.append(first * grad_x[a] + mixed * grad_y[a])
            flux_y.append(mixed * grad_x[a] + second * grad_y[a])
        weak = combine(table.T, flux_x)
        return [weak[a] + along(flux_y[a], backward) for a in range(4)]

    def keep(phase, lap, f, e, v, weak):
        for a in range(4):
            r = 4 * e + a
            lap[f, r + 1, pl.ds(v * SUB, SUB), :] = weak[a]
            if v == 0:
                send_w[phase, f, r] = weak[a][0:1]
            if v == tiles - 1:
                last = (cols - 1) % SUB
                send_e[phase, f, r] = weak[a][last : last + 1]

    def edge_copies(phase, lap, f):
        west, east = send_w.at[phase, f], send_e.at[phase, f]
        to_west, to_east = halo_e.at[phase, f], halo_w.at[phase, f]
        pairs = (
            (lap.at[f, 1], lap.at[f, rows + 1]),
            (lap.at[f, rows], lap.at[f, 0]),
            (west, to_west.at[pl.ds(1, rows)]),
            (east, to_east.at[pl.ds(1, rows)]),
            (west.at[0], to_west.at[rows + 1]),
            (east.at[0], to_east.at[rows + 1]),
            (west.at[rows - 1], to_west.at[0]),
            (east.at[rows - 1], to_east.at[0]),
        )
        return [
            pltpu.make_async_remote_copy(
                src_ref=source,
                dst_ref=target,
                send_sem=edge_send.at[phase, k, f],
                recv_sem=edge_recv.at[phase, k, f],
                device_id=partners[k],
                device_id_type=MESH,
            )
            for k, (source, target) in enumerate(pairs)
        ]

    low, high = mpad.at[pl.ds(0, SUB)], mpad.at[pl.ds(wide - SUB, SUB)]
    mass_pairs = (
        (low, mrow.at[1]), (high, mrow.at[0]),
        (mpad, mside.at[1]), (mpad, mside.at[0]),
        (low, mcorner.at[3]), (low, mcorner.at[2]),
        (high, mcorner.at[1]), (high, mcorner.at[0]),
    )
    mass_copies = [
        pltpu.make_async_remote_copy(
            src_ref=source,
            dst_ref=target,
            send_sem=mass_send.at[k],
            recv_sem=mass_recv.at[k],
            device_id=partners[k],
            device_id_type=MESH,
        )
        for k, (source, target) in enumerate(mass_pairs)
    ]

    def first_pass(f, carry):
        pltpu.make_async_copy(fields.at[f], u.at[f], load_sem.at[f]).wait()
        for e in range(blocks):
            for v in range(tiles):
                count = min(SUB, cols - v * SUB)
                values = []
                for a in range(4):
                    value = u[f, 4 * e + a, pl.ds(v * SUB, count), :]
                    if count < SUB:
                        value = lax.pad(value, np.float32(0), ((0, SUB - count, 0), (0, 0, 0)))
                    values.append(value)
                keep(0, lap1, f, e, v, laplace(values, e, v))
        return carry

    lax.fori_loop(0, nfield, first_pass, 0)

    pl.semaphore_wait(barrier, 8)
    for copy in mass_copies:
        copy.start()

    def send_first(f, carry):
        for copy in edge_copies(0, lap1, f):
            copy.start()
        return carry

    lax.fori_loop(0, nfield, send_first, 0)

    for copy in mass_copies:
        copy.wait_recv()
    rid = lax.broadcasted_iota(jnp.int32, (wide, LANES), 0)
    cid = lax.broadcasted_iota(jnp.int32, (wide, LANES), 1)
    zero = jnp.zeros((wide, LANES), jnp.float32)

    def down_rows(centre, north, south):
        total = centre
        inner_low = (rid % 4 == 0) & (rid > 0)
        inner_high = (rid % 4 == 3) & (rid < rows - 1)
        total = total + jnp.where(inner_low, pltpu.roll(centre, 1, 0), zero)
        total = total + jnp.where(inner_high, pltpu.roll(centre, wide - 1, 0), zero)
        before = jnp.broadcast_to(north, (wide, LANES))
        after = jnp.broadcast_to(south, (wide, LANES))
        total = total + jnp.where(rid == 0, before, zero)
        return total + jnp.where(rid == rows - 1, after, zero)

    last = (rows - 1) % SUB
    own = down_rows(mpad[...], mrow[0, last : last + 1], mrow[1, 0:1])
    west = down_rows(mside[0], mcorner[0, last : last + 1], mcorner[2, 0:1])
    east = down_rows(mside[1], mcorner[1, last : last + 1], mcorner[3, 0:1])
    total = own
    total = total + jnp.where((cid % 4 == 0) & (cid > 0), pltpu.roll(own, 1, 1), zero)
    total = total + jnp.where((cid % 4 == 3) & (cid < cols - 1), pltpu.roll(own, LANES - 1, 1), zero)
    total = total + jnp.where(cid == 0, pltpu.roll(west, LANES - cols + 1, 1), zero)
    total = total + jnp.where(cid == cols - 1, pltpu.roll(east, cols - 1, 1), zero)
    valid = (rid < rows) & (cid < cols)
    inverse = jnp.where(valid, 1.0 / jnp.where(valid, total, 1.0), 0.0)
    spread(3, jnp.concatenate([inverse, jnp.zeros((LANES - wide, LANES), jnp.float32)], axis=0))

    def assembled(phase, lap, f, r):
        parts = [lap[f, r + 1, pl.ds(v * SUB, SUB), :] for v in range(tiles)]
        side_w, side_e = halo_w[phase, f, r + 1], halo_e[phase, f, r + 1]
        other = None
        if r % 4 == 0:
            other = r
        elif r % 4 == 3:
            other = r + 2
        if other is not None:
            parts = [parts[v] + lap[f, other, pl.ds(v * SUB, SUB), :] for v in range(tiles)]
            side_w = side_w + halo_w[phase, f, other]
            side_e = side_e + halo_e[phase, f, other]
        prev = [pltpu.roll(x, 1, 0) for x in parts]
        nxt = [pltpu.roll(x, SUB - 1, 0) for x in parts]
        end = (cols - 1) % SUB
        out_tiles = []
        for v in range(tiles):
            before = jnp.broadcast_to(side_w, (SUB, LANES)) if v == 0 else prev[v - 1]
            add = jnp.where(sub == 0, before, jnp.where(sub == 4, prev[v], 0.0))
            if v < tiles - 1:
                add = jnp.where(sub == 3, nxt[v], jnp.where(sub == 7, nxt[v + 1], add))
            else:
                after = jnp.broadcast_to(side_e, (SUB, LANES))
                if end == 7:
                    add = jnp.where(sub == 3, nxt[v], add)
                add = jnp.where(sub == end, after, add)
            out_tiles.append((parts[v] + add) * weights[3, r, pl.ds(v * SUB, SUB), :])
        return out_tiles

    def second_pass(f, carry):
        for copy in edge_copies(0, lap1, f):
            copy.wait_recv()
        for e in range(blocks):
            values = [assembled(0, lap1, f, 4 * e + a) for a in range(4)]
            for v in range(tiles):
                weak = laplace([values[a][v] for a in range(4)], e, v)
                keep(1, lap2, f, e, v, weak)
        for copy in edge_copies(1, lap2, f):
            copy.start()
        return carry

    lax.fori_loop(0, nfield, second_pass, 0)

    def last_pass(f, carry):
        for copy in edge_copies(1, lap2, f):
            copy.wait_recv()
        for r in range(rows):
            done = assembled(1, lap2, f, r)
            for v in range(tiles):
                count = min(SUB, cols - v * SUB)
                result[f, r, pl.ds(v * SUB, count), :] = done[v][:count]
        pltpu.make_async_copy(result.at[f], out.at[f], store_sem.at[f]).start()
        return carry

    lax.fori_loop(0, nfield, last_pass, 0)

    def finish(f, carry):
        for copy in edge_copies(0, lap1, f) + edge_copies(1, lap2, f):
            copy.wait_send()
        pltpu.make_async_copy(result.at[f], out.at[f], store_sem.at[f]).wait()
        return carry

    for copy in mass_copies:
        copy.wait_send()
    lax.fori_loop(0, nfield, finish, 0)


def solution(mesh):
    faces, cols_axis = mesh.shape["face"], mesh.shape["col"]

    def shards(fields, metric_diag, metric_cross, point_mass):
        nfield, rows, cols, lanes = fields.shape
        wide = -(-cols // SUB) * SUB
        f32 = jnp.float32
        anywhere = pl.BlockSpec(memory_space=pl.ANY)
        return pl.pallas_call(
            functools.partial(operator_kernel, faces, cols_axis, nfield, rows, cols),
            out_shape=jax.ShapeDtypeStruct(fields.shape, f32),
            in_specs=[anywhere] * 4,
            out_specs=anywhere,
            scratch_shapes=[
                pltpu.VMEM((nfield, rows, cols, lanes), f32),
                pltpu.VMEM((2, rows, cols), f32),
                pltpu.VMEM((rows, cols), f32),
                pltpu.VMEM((rows, cols), f32),
                pltpu.VMEM((wide, LANES), f32),
                pltpu.VMEM((2, SUB, LANES), f32),
                pltpu.VMEM((2, wide, LANES), f32),
                pltpu.VMEM((4, SUB, LANES), f32),
                pltpu.VMEM((4, rows, wide, LANES), f32),
                pltpu.VMEM((nfield, rows + 2, wide, lanes), f32),
                pltpu.VMEM((nfield, rows + 2, wide, lanes), f32),
                pltpu.VMEM((2, nfield, rows, 1, lanes), f32),
                pltpu.VMEM((2, nfield, rows, 1, lanes), f32),
                pltpu.VMEM((2, nfield, rows + 2, 1, lanes), f32),
                pltpu.VMEM((2, nfield, rows + 2, 1, lanes), f32),
                pltpu.VMEM((nfield, rows, cols, lanes), f32),
                pltpu.SemaphoreType.DMA((nfield + 3,)),
                pltpu.SemaphoreType.DMA((nfield,)),
                pltpu.SemaphoreType.DMA((8,)),
                pltpu.SemaphoreType.DMA((8,)),
                pltpu.SemaphoreType.DMA((2, 8, nfield)),
                pltpu.SemaphoreType.DMA((2, 8, nfield)),
            ],
            compiler_params=pltpu.CompilerParams(collective_id=0, has_side_effects=True),
        )(fields, metric_diag, metric_cross, point_mass)

    return jax.shard_map(
        shards,
        mesh=mesh,
        in_specs=(
            P(None, "face", "col", None),
            P(None, "face", "col"),
            P("face", "col"),
            P("face", "col"),
        ),
        out_specs=P(None, "face", "col", None),
        check_vma=False,
    )
```

time: 105 us -> 48.1 us (0.46)
  the two profiles are of different devices: /device:TPU:7 before, /device:TPU:1 now
where the time goes in v1:
time: 48.1 us; the launch traced here: 47.8 us
  Pallas kernels  41.6 us (86%)
  local copies, waits for them, and re-layouts  6.14 us (13%)
    pallas_call x1, Pallas kernels, shards(): pl.pallas_call(functools.partial(operator_kernel, faces, cols_axis, nfiel...  41.6 us
    unnamed x2, local copies, waits for them, and re-layouts  3.52 us
    pallas_call x1, local copies, waits for them, and re-layouts, shards(): pl.pallas_call(functools.partial(operator_kernel, faces, cols_axis, nfiel...  2.62 us

profile of v1, /device:TPU:1, one launch (start us, length us, event | category | flops | bytes accessed | tf_op | source)
XLA Modules:
  0.0 47.8 jit_solution(5514532840214201469)
XLA Ops:
  0.0 1.3 %copy.6.diag = f32[2,20,20]{2,1,0:T(8,128)} copy(f32[2,20,20]{2,0,1:T(2,128)} %param.5) | data formatting | bytes 6400 | tf_op args[1]
  1.3 2.2 %copy.5.fields = f32[4,20,20,128]{3,2,1,0:T(8,128)} copy(f32[4,20,20,128]{3,0,2,1:T(4,128)} %param.4) | data formatting | bytes 1638400 | tf_op args[0]
  3.5 41.6 %shard_map.46 = f32[4,20,20,128]{3,2,1,0:T(8,128)} custom-call(f32[4,20,20,128]{3,2,1,0:T(8,128)} %copy.5.fields, f32[2,20,20]{2,1,0:T(8,128)} %copy.6.diag, f32[20,20]{1,0:T(8,128)} %cross.1, f32[20,20]{1,0:T(8,128)} %mass.1), custom_call_target="tpu_custom_call" | custom-call | tf_op jit(solution)/shard_map/pallas_call | solution.py:320
  45.2 2.6 %copy.7 = f32[4,20,20,128]{3,0,2,1:T(4,128)} copy(f32[4,20,20,128]{3,2,1,0:T(8,128)} %shard_map.46) | data formatting | bytes 1638400 | tf_op jit(solution)/shard_map/pallas_call | solution.py:320

commit v2 on v1

v2 whole, which is shorter than its diff:
```python
import functools

import jax
import jax.numpy as jnp
import numpy as np
from jax import lax
from jax.experimental import pallas as pl
from jax.experimental.pallas import tpu as pltpu
from jax.sharding import PartitionSpec as P

MESH = pl.DeviceIdType.MESH
SUB = 8
LANES = 128


def derivative_table():
    small = 1.0 / np.sqrt(5.0)
    nodes = np.array([-1.0, -small, small, 1.0])
    count = nodes.shape[0]
    weights = np.array(
        [np.prod([nodes[a] - nodes[k] for k in range(count) if k != a]) for a in range(count)]
    )
    table = np.zeros((count, count))
    for a in range(count):
        for b in range(count):
            if a == b:
                table[a, b] = np.sum([1.0 / (nodes[a] - nodes[k]) for k in range(count) if k != a])
            else:
                table[a, b] = weights[a] / weights[b] / (nodes[a] - nodes[b])
    table[np.abs(table) < 1e-12] = 0.0
    return table


def combine(table, parts):
    out = []
    for a in range(4):
        total = None
        for b in range(4):
            if table[a, b] == 0.0:
                continue
            term = np.float32(table[a, b]) * parts[b]
            total = term if total is None else total + term
        out.append(total)
    return out


def pair_coefficients(table):
    high = lax.broadcasted_iota(jnp.int32, (SUB, LANES), 0) >= SUB // 2
    result = []
    for p in range(2):
        line = []
        for q in range(2):
            kept = jnp.where(high, np.float32(table[2 * p + 1, 2 * q + 1]), np.float32(table[2 * p, 2 * q]))
            swapped = jnp.where(high, np.float32(table[2 * p + 1, 2 * q]), np.float32(table[2 * p, 2 * q + 1]))
            line.append((kept, swapped))
        result.append(line)
    return result


def swap(tile):
    return pltpu.roll(tile, SUB // 2, 0)


def along(pair, coefficients):
    turned = [swap(x) for x in pair]
    out = []
    for p in range(2):
        total = None
        for q in range(2):
            kept, swapped = coefficients[p][q]
            term = kept * pair[q] + swapped * turned[q]
            total = term if total is None else total + term
        out.append(total)
    return out


def operator_kernel(
    faces, cols_axis, rows, cols,
    fields, diag, cross, mass,
    out,
    u, md, mc, mp, mpad, mrow, mside, mcorner, column, weights, lap1, lap2,
    load_sem, mass_send, mass_recv, edge_send, edge_recv,
):
    table = derivative_table()
    blocks_x, blocks_y = rows // 4, cols // 4
    pairs = cols // 2
    wide = -(-cols // SUB) * SUB
    face = lax.axis_index("face")
    col = lax.axis_index("col")
    up, down = lax.rem(face + faces - 1, faces), lax.rem(face + 1, faces)
    left, right = lax.rem(col + cols_axis - 1, cols_axis), lax.rem(col + 1, cols_axis)
    partners = (
        (up, col), (down, col), (face, left), (face, right),
        (up, left), (up, right), (down, left), (down, right),
    )

    barrier = pltpu.get_barrier_semaphore()
    for partner in partners:
        pl.semaphore_signal(barrier, inc=1, device_id=partner, device_id_type=MESH)

    small_loads = [
        pltpu.make_async_copy(source, target, load_sem.at[blocks_x + k])
        for k, (source, target) in enumerate(((diag, md), (cross, mc), (mass, mp)))
    ]

    def field_load(e):
        window = pl.ds(4 * e, 4)
        return pltpu.make_async_copy(fields.at[window], u.at[window], load_sem.at[e])

    for load in small_loads:
        load.start()
    for e in range(blocks_x):
        field_load(e).start()

    high = lax.broadcasted_iota(jnp.int32, (SUB, LANES), 0) >= SUB // 2

    def spread(k, square):
        turned = jnp.transpose(square)
        for r in range(rows):
            column[k, r] = jnp.broadcast_to(turned[:wide, r : r + 1], (wide, LANES))

        def pair_up(r, carry):
            for p in range(pairs):
                one = jnp.broadcast_to(column[k, r, pl.ds(2 * p, 1), :], (SUB, LANES))
                two = jnp.broadcast_to(column[k, r, pl.ds(2 * p + 1, 1), :], (SUB, LANES))
                weights[k, r, p] = jnp.where(high, two, one)
            return carry

        lax.fori_loop(0, rows, pair_up, 0)

    def padded(value):
        return lax.pad(value, np.float32(0), ((0, LANES - rows, 0), (0, LANES - cols, 0)))

    for load in small_loads:
        load.wait()
    mpad[...] = padded(mp[...])[:wide]
    spread(0, padded(md[:, 0, :]))
    spread(1, padded(md[:, 1, :]))
    spread(2, padded(mc[...]))

    forward = pair_coefficients(table)
    backward = pair_coefficients(table.T)

    def laplace(values, e, g):
        grad_x = [combine(table, [values[a][q] for a in range(4)]) for q in range(2)]
        flux_x, flux_y = [[], []], []
        for a in range(4):
            grad_y = along(values[a], forward)
            line = []
            for q in range(2):
                first, second, mixed = (weights[k, 4 * e + a, 2 * g + q] for k in range(3))
                flux_x[q].append(first * grad_x[q][a] + mixed * grad_y[q])
                line.append(mixed * grad_x[q][a] + second * grad_y[q])
            flux_y.append(line)
        weak = [combine(table.T, flux_x[q]) for q in range(2)]
        for a in range(4):
            other = along(flux_y[a], backward)
            for q in range(2):
                weak[q][a] = weak[q][a] + other[q]
        return weak

    def keep(lap, e, g, weak):
        for a in range(4):
            for q in range(2):
                lap[4 * e + a + 1, 2 * g + q + 1] = weak[q][a]

    half = SUB // 2
    low_half, high_half = pl.ds(0, half), pl.ds(half, half)

    def edge_copies(phase, lap):
        inner, across = pl.ds(1, rows), pl.ds(1, pairs)
        moves = (
            (lap.at[1, across], lap.at[rows + 1, across]),
            (lap.at[rows, across], lap.at[0, across]),
            (lap.at[inner, 1, low_half], lap.at[inner, pairs + 1, low_half]),
            (lap.at[inner, pairs, high_half], lap.at[inner, 0, high_half]),
            (lap.at[1, 1, low_half], lap.at[rows + 1, pairs + 1, low_half]),
            (lap.at[1, pairs, high_half], lap.at[rows + 1, 0, high_half]),
            (lap.at[rows, 1, low_half], lap.at[0, pairs + 1, low_half]),
            (lap.at[rows, pairs, high_half], lap.at[0, 0, high_half]),
        )
        return [
            pltpu.make_async_remote_copy(
                src_ref=source,
                dst_ref=target,
                send_sem=edge_send.at[phase, k],
                recv_sem=edge_recv.at[phase, k],
                device_id=partners[k],
                device_id_type=MESH,
            )
            for k, (source, target) in enumerate(moves)
        ]

    top, bottom = mpad.at[pl.ds(0, SUB)], mpad.at[pl.ds(wide - SUB, SUB)]
    mass_moves = (
        (top, mrow.at[1]), (bottom, mrow.at[0]),
        (mpad, mside.at[1]), (mpad, mside.at[0]),
        (top, mcorner.at[3]), (top, mcorner.at[2]),
        (bottom, mcorner.at[1]), (bottom, mcorner.at[0]),
    )
    mass_copies = [
        pltpu.make_async_remote_copy(
            src_ref=source,
            dst_ref=target,
            send_sem=mass_send.at[k],
            recv_sem=mass_recv.at[k],
            device_id=partners[k],
            device_id_type=MESH,
        )
        for k, (source, target) in enumerate(mass_moves)
    ]

    def first_pass(e, carry):
        field_load(e).wait()
        for g in range(blocks_y):
            values = [[u[4 * e + a, 2 * g + q] for q in range(2)] for a in range(4)]
            keep(lap1, e, g, laplace(values, e, g))
        return carry

    lax.fori_loop(0, blocks_x, first_pass, 0)

    pl.semaphore_wait(barrier, 8)
    first_copies = edge_copies(0, lap1)
    for copy in mass_copies + first_copies:
        copy.start()

    for copy in mass_copies:
        copy.wait_recv()
    rid = lax.broadcasted_iota(jnp.int32, (wide, LANES), 0)
    cid = lax.broadcasted_iota(jnp.int32, (wide, LANES), 1)
    zero = jnp.zeros((wide, LANES), jnp.float32)

    def down_rows(centre, north, south):
        total = centre
        inner_low = (rid % 4 == 0) & (rid > 0)
        inner_high = (rid % 4 == 3) & (rid < rows - 1)
        total = total + jnp.where(inner_low, pltpu.roll(centre, 1, 0), zero)
        total = total + jnp.where(inner_high, pltpu.roll(centre, wide - 1, 0), zero)
        before = jnp.broadcast_to(north, (wide, LANES))
        after = jnp.broadcast_to(south, (wide, LANES))
        total = total + jnp.where(rid == 0, before, zero)
        return total + jnp.where(rid == rows - 1, after, zero)

    last = (rows - 1) % SUB
    own = down_rows(mpad[...], mrow[0, last : last + 1], mrow[1, 0:1])
    west = down_rows(mside[0], mcorner[0, last : last + 1], mcorner[2, 0:1])
    east = down_rows(mside[1], mcorner[1, last : last + 1], mcorner[3, 0:1])
    total = own
    total = total + jnp.where((cid % 4 == 0) & (cid > 0), pltpu.roll(own, 1, 1), zero)
    total = total + jnp.where((cid % 4 == 3) & (cid < cols - 1), pltpu.roll(own, LANES - 1, 1), zero)
    total = total + jnp.where(cid == 0, pltpu.roll(west, LANES - cols + 1, 1), zero)
    total = total + jnp.where(cid == cols - 1, pltpu.roll(east, cols - 1, 1), zero)
    valid = (rid < rows) & (cid < cols)
    inverse = jnp.where(valid, 1.0 / jnp.where(valid, total, 1.0), 0.0)
    spread(3, jnp.concatenate([inverse, jnp.zeros((LANES - wide, LANES), jnp.float32)], axis=0))

    def assembled(lap, e, a):
        r = 4 * e + a
        parts = [lap[r + 1, p] for p in range(pairs + 2)]
        if a == 0:
            parts = [parts[p] + lap[r, p] for p in range(pairs + 2)]
        if a == 3:
            parts = [parts[p] + lap[r + 2, p] for p in range(pairs + 2)]
        tiles = []
        for p in range(pairs):
            if p % 2 == 0:
                add = jnp.where(high, 0.0, swap(parts[p]))
            else:
                add = jnp.where(high, swap(parts[p + 2]), 0.0)
            tiles.append((parts[p + 1] + add) * weights[3, r, p])
        return tiles

    for copy in first_copies:
        copy.wait_recv()

    def second_pass(e, carry):
        values = [assembled(lap1, e, a) for a in range(4)]
        for g in range(blocks_y):
            keep(lap2, e, g, laplace([[values[a][2 * g + q] for q in range(2)] for a in range(4)], e, g))
        return carry

    lax.fori_loop(0, blocks_x, second_pass, 0)

    second_copies = edge_copies(1, lap2)
    for copy in second_copies:
        copy.start()
    for copy in second_copies:
        copy.wait_recv()

    def last_pass(e, carry):
        for a in range(4):
            done = assembled(lap2, e, a)
            for p in range(pairs):
                out[4 * e + a, p] = done[p]
        return carry

    lax.fori_loop(0, blocks_x, last_pass, 0)

    for copy in mass_copies + first_copies + second_copies:
        copy.wait_send()


def solution(mesh):
    faces, cols_axis = mesh.shape["face"], mesh.shape["col"]

    def shards(fields, metric_diag, metric_cross, point_mass):
        nfield, rows, cols, lanes = fields.shape
        wide = -(-cols // SUB) * SUB
        pairs = cols // 2
        f32 = jnp.float32
        anywhere = pl.BlockSpec(memory_space=pl.ANY)
        tiles = fields.transpose(1, 2, 0, 3).reshape(rows, pairs, 2 * nfield, lanes)
        result = pl.pallas_call(
            functools.partial(operator_kernel, faces, cols_axis, rows, cols),
            out_shape=pltpu.VMEM((rows, pairs, 2 * nfield, lanes), f32),
            in_specs=[anywhere] * 4,
            out_specs=pl.BlockSpec(memory_space=pltpu.VMEM),
            scratch_shapes=[
                pltpu.VMEM((rows, pairs, SUB, lanes), f32),
                pltpu.VMEM((rows, 2, cols), f32),
                pltpu.VMEM((rows, cols), f32),
                pltpu.VMEM((rows, cols), f32),
                pltpu.VMEM((wide, LANES), f32),
                pltpu.VMEM((2, SUB, LANES), f32),
                pltpu.VMEM((2, wide, LANES), f32),
                pltpu.VMEM((4, SUB, LANES), f32),
                pltpu.VMEM((4, rows, wide, LANES), f32),
                pltpu.VMEM((4, rows, pairs, SUB, LANES), f32),
                pltpu.VMEM((rows + 2, pairs + 2, SUB, lanes), f32),
                pltpu.VMEM((rows + 2, pairs + 2, SUB, lanes), f32),
                pltpu.SemaphoreType.DMA((rows // 4 + 3,)),
                pltpu.SemaphoreType.DMA((8,)),
                pltpu.SemaphoreType.DMA((8,)),
                pltpu.SemaphoreType.DMA((2, 8)),
                pltpu.SemaphoreType.DMA((2, 8)),
            ],
            compiler_params=pltpu.CompilerParams(collective_id=0, has_side_effects=True),
        )(tiles, metric_diag.transpose(1, 0, 2), metric_cross, point_mass)
        return result.reshape(rows, cols, nfield, lanes).transpose(2, 0, 1, 3)

    return jax.shard_map(
        shards,
        mesh=mesh,
        in_specs=(
            P(None, "face", "col", None),
            P(None, "face", "col"),
            P("face", "col"),
            P("face", "col"),
        ),
        out_specs=P(None, "face", "col", None),
        check_vma=False,
    )
```

time: 48.1 us -> 41.8 us (0.87)
  local copies, waits for them, and re-layouts: 6.14 us -> 0.89 us
  Pallas kernels: 41.6 us -> 40.7 us
    unnamed x2 -> x1, local copies, waits for them, and re-layouts: 3.52 us -> 0.89 us
    pallas_call x1 -> x0, local copies, waits for them, and re-layouts: 2.62 us -> none  [shards(): pl.pallas_call(functools.partial(operator_kernel, faces, cols_axis, nfiel...]
    pallas_call x1, Pallas kernels: 41.6 us -> 40.7 us  [shards(): pl.pallas_call(functools.partial(operator_kernel, faces, cols_axis, rows,...]
where the time goes in v2:
time: 41.8 us; the launch traced here: 41.6 us
  Pallas kernels  40.7 us (97%)
  local copies, waits for them, and re-layouts  0.89 us (2%)
    pallas_call x1, Pallas kernels, shards(): pl.pallas_call(functools.partial(operator_kernel, faces, cols_axis, rows,...  40.7 us
    unnamed x1, local copies, waits for them, and re-layouts  0.89 us

profile of v2, /device:TPU:1, one launch (start us, length us, event | category | flops | bytes accessed | tf_op | source)
XLA Modules:
  0.0 41.6 jit_solution(1515509036086391880)
XLA Ops:
  0.0 40.7 %shard_map.46 = f32[20,10,8,128]{3,2,1,0:T(8,128)S(1)} custom-call(f32[20,10,8,128]{3,2,1,0:T(8,128)} %bitcast.8, f32[20,2,20]{2,1,0:T(2,128)} %bitcast.9, f32[20,20]{1,0:T(8,128)} %cross.1, f32[20,20]{1,0:T(8,128)} %mass.1), custom_call_target="tpu_custom_call" | custom-call | tf_op jit(solution)/shard_map/pallas_call | solution.py:313
  40.8 0.9 %copy.6 = f32[4,20,20,128]{3,0,2,1:T(4,128)} copy(f32[4,20,20,128]{3,0,2,1:T(4,128)S(1)} %bitcast.7) | data formatting | bytes 1638400

commit v3 on v2

--- a/solution.py
+++ b/solution.py
@@ -114,29 +114,48 @@
 
     high = lax.broadcasted_iota(jnp.int32, (SUB, LANES), 0) >= SUB // 2
 
-    def spread(k, square):
-        turned = jnp.transpose(square)
+    def pair_tile(k, r, p):
+        one = jnp.broadcast_to(column[k, r, pl.ds(2 * p, 1), :], (SUB, LANES))
+        two = jnp.broadcast_to(column[k, r, pl.ds(2 * p + 1, 1), :], (SUB, LANES))
+        weights[k, r, p] = jnp.where(high, two, one)
+
+    def spread(k, turned):
         for r in range(rows):
-            column[k, r] = jnp.broadcast_to(turned[:wide, r : r + 1], (wide, LANES))
+            column[k, r] = jnp.broadcast_to(turned[:, r : r + 1], (wide, LANES))
 
         def pair_up(r, carry):
             for p in range(pairs):
-                one = jnp.broadcast_to(column[k, r, pl.ds(2 * p, 1), :], (SUB, LANES))
-                two = jnp.broadcast_to(column[k, r, pl.ds(2 * p + 1, 1), :], (SUB, LANES))
-                weights[k, r, p] = jnp.where(high, two, one)
+                pair_tile(k, r, p)
             return carry
 
         lax.fori_loop(0, rows, pair_up, 0)
 
-    def padded(value):
-        return lax.pad(value, np.float32(0), ((0, LANES - rows, 0), (0, LANES - cols, 0)))
+    def turned(value):
+        square = lax.pad(value, np.float32(0), ((0, LANES - rows, 0), (0, LANES - cols, 0)))
+        return jnp.transpose(square)[:wide]
+
+    cid = lax.broadcasted_iota(jnp.int32, (wide, LANES), 0)
+    rid = lax.broadcasted_iota(jnp.int32, (wide, LANES), 1)
+    zero = jnp.zeros((wide, LANES), jnp.float32)
+    valid = (rid < rows) & (cid < cols)
+
+    def over_columns(centre):
+        total = centre + jnp.where((cid % 4 == 0) & (cid > 0), pltpu.roll(centre, 1, 0), zero)
+        return total + jnp.where((cid % 4 == 3) & (cid < cols - 1), pltpu.roll(centre, wide - 1, 0), zero)
+
+    def over_rows(centre):
+        total = centre + jnp.where((rid % 4 == 0) & (rid > 0), pltpu.roll(centre, 1, 1), zero)
+        return total + jnp.where((rid % 4 == 3) & (rid < rows - 1), pltpu.roll(centre, LANES - 1, 1), zero)
+
+    def inverse(total):
+        return jnp.where(valid, 1.0 / jnp.where(valid, total, 1.0), 0.0)
 
     for load in small_loads:
         load.wait()
-    mpad[...] = padded(mp[...])[:wide]
-    spread(0, padded(md[:, 0, :]))
-    spread(1, padded(md[:, 1, :]))
-    spread(2, padded(mc[...]))
+    mpad[...] = turned(mp[...])
+    spread(0, turned(md[:, 0, :]))
+    spread(1, turned(md[:, 1, :]))
+    spread(2, turned(mc[...]))
 
     forward = pair_coefficients(table)
     backward = pair_coefficients(table.T)
@@ -167,6 +186,16 @@
     half = SUB // 2
     low_half, high_half = pl.ds(0, half), pl.ds(half, half)
 
+    def remote(source, target, k, send_sem, recv_sem):
+        return pltpu.make_async_remote_copy(
+            src_ref=source,
+            dst_ref=target,
+            send_sem=send_sem,
+            recv_sem=recv_sem,
+            device_id=partners[k],
+            device_id_type=MESH,
+        )
+
     def edge_copies(phase, lap):
         inner, across = pl.ds(1, rows), pl.ds(1, pairs)
         moves = (
@@ -180,33 +209,19 @@
             (lap.at[rows, pairs, high_half], lap.at[0, 0, high_half]),
         )
         return [
-            pltpu.make_async_remote_copy(
-                src_ref=source,
-                dst_ref=target,
-                send_sem=edge_send.at[phase, k],
-                recv_sem=edge_recv.at[phase, k],
-                device_id=partners[k],
-                device_id_type=MESH,
-            )
+            remote(source, target, k, edge_send.at[phase, k], edge_recv.at[phase, k])
             for k, (source, target) in enumerate(moves)
         ]
 
-    top, bottom = mpad.at[pl.ds(0, SUB)], mpad.at[pl.ds(wide - SUB, SUB)]
+    left_tile, right_tile = mpad.at[pl.ds(0, SUB)], mpad.at[pl.ds(wide - SUB, SUB)]
     mass_moves = (
-        (top, mrow.at[1]), (bottom, mrow.at[0]),
         (mpad, mside.at[1]), (mpad, mside.at[0]),
-        (top, mcorner.at[3]), (top, mcorner.at[2]),
-        (bottom, mcorner.at[1]), (bottom, mcorner.at[0]),
+        (left_tile, mrow.at[1]), (right_tile, mrow.at[0]),
+        (left_tile, mcorner.at[3]), (right_tile, mcorner.at[2]),
+        (left_tile, mcorner.at[1]), (right_tile, mcorner.at[0]),
     )
     mass_copies = [
-        pltpu.make_async_remote_copy(
-            src_ref=source,
-            dst_ref=target,
-            send_sem=mass_send.at[k],
-            recv_sem=mass_recv.at[k],
-            device_id=partners[k],
-            device_id_type=MESH,
-        )
+        remote(source, target, k, mass_send.at[k], mass_recv.at[k])
         for k, (source, target) in enumerate(mass_moves)
     ]
 
@@ -219,82 +234,124 @@
 
     lax.fori_loop(0, blocks_x, first_pass, 0)
 
+    spread(3, inverse(over_rows(over_columns(mpad[...]))))
+
     pl.semaphore_wait(barrier, 8)
     first_copies = edge_copies(0, lap1)
-    for copy in mass_copies + first_copies:
+    for copy in first_copies[4:] + mass_copies[4:] + mass_copies[2:4] + first_copies[2:4] + mass_copies[:2] + first_copies[:2]:
         copy.start()
+
+    def assembled(lap, e, a, window):
+        r = 4 * e + a
+
+        def summed(p):
+            part = lap[r + 1, p + 1]
+            if a == 0:
+                part = part + lap[r, p + 1]
+            if a == 3:
+                part = part + lap[r + 2, p + 1]
+            return part
+
+        parts = {}
+        tiles = []
+        for p in window:
+            other = p - 1 if p % 2 == 0 else p + 1
+            for q in (p, other):
+                if q not in parts:
+                    parts[q] = summed(q)
+            turn = swap(parts[other])
+            add = jnp.where(high, 0.0, turn) if p % 2 == 0 else jnp.where(high, turn, 0.0)
+            tiles.append((parts[p] + add) * weights[3, r, p])
+        return tiles
+
+    def second(e, g):
+        values = [assembled(lap1, e, a, (2 * g, 2 * g + 1)) for a in range(4)]
+        keep(lap2, e, g, laplace(values, e, g))
+
+    inner_blocks = range(1, blocks_y - 1)
+    rim_blocks = (0, blocks_y - 1)
+
+    def loop(low, high_end, body):
+        def step(i, carry):
+            body(i)
+            return carry
+
+        lax.fori_loop(low, high_end, step, 0)
+
+    def over(blocks):
+        def body(e):
+            for g in blocks:
+                second(e, g)
+
+        return body
+
+    loop(1, blocks_x - 1, over(inner_blocks))
 
     for copy in mass_copies:
         copy.wait_recv()
-    rid = lax.broadcasted_iota(jnp.int32, (wide, LANES), 0)
-    cid = lax.broadcasted_iota(jnp.int32, (wide, LANES), 1)
-    zero = jnp.zeros((wide, LANES), jnp.float32)
-
-    def down_rows(centre, north, south):
-        total = centre
-        inner_low = (rid % 4 == 0) & (rid > 0)
-        inner_high = (rid % 4 == 3) & (rid < rows - 1)
-        total = total + jnp.where(inner_low, pltpu.roll(centre, 1, 0), zero)
-        total = total + jnp.where(inner_high, pltpu.roll(centre, wide - 1, 0), zero)
-        before = jnp.broadcast_to(north, (wide, LANES))
-        after = jnp.broadcast_to(south, (wide, LANES))
-        total = total + jnp.where(rid == 0, before, zero)
-        return total + jnp.where(rid == rows - 1, after, zero)
-
-    last = (rows - 1) % SUB
-    own = down_rows(mpad[...], mrow[0, last : last + 1], mrow[1, 0:1])
-    west = down_rows(mside[0], mcorner[0, last : last + 1], mcorner[2, 0:1])
-    east = down_rows(mside[1], mcorner[1, last : last + 1], mcorner[3, 0:1])
-    total = own
-    total = total + jnp.where((cid % 4 == 0) & (cid > 0), pltpu.roll(own, 1, 1), zero)
-    total = total + jnp.where((cid % 4 == 3) & (cid < cols - 1), pltpu.roll(own, LANES - 1, 1), zero)
-    total = total + jnp.where(cid == 0, pltpu.roll(west, LANES - cols + 1, 1), zero)
-    total = total + jnp.where(cid == cols - 1, pltpu.roll(east, cols - 1, 1), zero)
-    valid = (rid < rows) & (cid < cols)
-    inverse = jnp.where(valid, 1.0 / jnp.where(valid, total, 1.0), 0.0)
-    spread(3, jnp.concatenate([inverse, jnp.zeros((LANES - wide, LANES), jnp.float32)], axis=0))
-
-    def assembled(lap, e, a):
-        r = 4 * e + a
-        parts = [lap[r + 1, p] for p in range(pairs + 2)]
-        if a == 0:
-            parts = [parts[p] + lap[r, p] for p in range(pairs + 2)]
-        if a == 3:
-            parts = [parts[p] + lap[r + 2, p] for p in range(pairs + 2)]
-        tiles = []
-        for p in range(pairs):
-            if p % 2 == 0:
-                add = jnp.where(high, 0.0, swap(parts[p]))
-            else:
-                add = jnp.where(high, swap(parts[p + 2]), 0.0)
-            tiles.append((parts[p + 1] + add) * weights[3, r, p])
-        return tiles
+
+    def with_ends(centre, before, after):
+        total = over_columns(centre)
+        total = total + jnp.where(cid == 0, jnp.broadcast_to(before, (wide, LANES)), zero)
+        return total + jnp.where(cid == cols - 1, jnp.broadcast_to(after, (wide, LANES)), zero)
+
+    last = (cols - 1) % SUB
+    own = with_ends(mpad[...], mrow[0, last : last + 1], mrow[1, 0:1])
+    north = with_ends(mside[0], mcorner[0, last : last + 1], mcorner[1, 0:1])
+    south = with_ends(mside[1], mcorner[2, last : last + 1], mcorner[3, 0:1])
+    total = over_rows(own)
+    total = total + jnp.where(rid == 0, pltpu.roll(north, LANES - rows + 1, 1), zero)
+    total = total + jnp.where(rid == rows - 1, pltpu.roll(south, rows - 1, 1), zero)
+    full = inverse(total)
+    for r in range(rows):
+        if r in (0, rows - 1):
+            column[3, r] = jnp.broadcast_to(full[:, r : r + 1], (wide, LANES))
+            for p in range(pairs):
+                pair_tile(3, r, p)
+        else:
+            for p in (0, pairs - 1):
+                start = 2 * p // SUB * SUB
+                column[3, r, pl.ds(start, SUB), :] = jnp.broadcast_to(full[start : start + SUB, r : r + 1], (SUB, LANES))
+                pair_tile(3, r, p)
 
     for copy in first_copies:
         copy.wait_recv()
 
-    def second_pass(e, carry):
-        values = [assembled(lap1, e, a) for a in range(4)]
-        for g in range(blocks_y):
-            keep(lap2, e, g, laplace([[values[a][2 * g + q] for q in range(2)] for a in range(4)], e, g))
-        return carry
-
-    lax.fori_loop(0, blocks_x, second_pass, 0)
-
     second_copies = edge_copies(1, lap2)
-    for copy in second_copies:
+    loop(0, 2, lambda i: over(rim_blocks)(i * (blocks_x - 1)))
+    for copy in second_copies[4:]:
         copy.start()
+    loop(1, blocks_x - 1, over(rim_blocks))
+    for copy in second_copies[2:4]:
+        copy.start()
+    loop(0, 2, lambda i: over(inner_blocks)(i * (blocks_x - 1)))
+    for copy in second_copies[:2]:
+        copy.start()
+
+    def write(e, a, window):
+        for p, tile in zip(window, assembled(lap2, e, a, window)):
+            out[4 * e + a, p] = tile
+
+    middle, rim = tuple(range(1, pairs - 1)), (0, pairs - 1)
+
+    def write_rows(window):
+        for a in range(1, 4):
+            write(0, a, window)
+        for a in range(3):
+            write(blocks_x - 1, a, window)
+
+        def body(e):
+            for a in range(4):
+                write(e, a, window)
+
+        loop(1, blocks_x - 1, body)
+
+    write_rows(middle)
     for copy in second_copies:
         copy.wait_recv()
-
-    def last_pass(e, carry):
-        for a in range(4):
-            done = assembled(lap2, e, a)
-            for p in range(pairs):
-                out[4 * e + a, p] = done[p]
-        return carry
-
-    lax.fori_loop(0, blocks_x, last_pass, 0)
+    write_rows(rim)
+    write(0, 0, tuple(range(pairs)))
+    write(blocks_x - 1, 3, tuple(range(pairs)))
 
     for copy in mass_copies + first_copies + second_copies:
         copy.wait_send()

time: 41.8 us -> 37.6 us (0.90)
  the two profiles are of different devices: /device:TPU:1 before, /device:TPU:8 now
where the time goes in v3:
time: 37.6 us; the launch traced here: 37.4 us
  Pallas kernels  36.5 us (97%)
  local copies, waits for them, and re-layouts  0.89 us (2%)
    pallas_call x1, Pallas kernels, shards(): pl.pallas_call(functools.partial(operator_kernel, faces, cols_axis, rows,...  36.5 us
    unnamed x1, local copies, waits for them, and re-layouts  0.89 us

profile of v3, /device:TPU:8, one launch (start us, length us, event | category | flops | bytes accessed | tf_op | source)
XLA Modules:
  0.0 37.4 jit_solution(8261845890497913421)
XLA Ops:
  0.0 36.5 %shard_map.46 = f32[20,10,8,128]{3,2,1,0:T(8,128)S(1)} custom-call(f32[20,10,8,128]{3,2,1,0:T(8,128)} %bitcast.8, f32[20,2,20]{2,1,0:T(2,128)} %bitcast.9, f32[20,20]{1,0:T(8,128)} %cross.1, f32[20,20]{1,0:T(8,128)} %mass.1), custom_call_target="tpu_custom_call" | custom-call | tf_op jit(solution)/shard_map/pallas_call | solution.py:370
  36.5 0.9 %copy.6 = f32[4,20,20,128]{3,0,2,1:T(4,128)} copy(f32[4,20,20,128]{3,0,2,1:T(4,128)S(1)} %bitcast.7) | data formatting | bytes 1638400

commit v4 on v3

--- a/solution.py
+++ b/solution.py
@@ -213,6 +213,27 @@
             for k, (source, target) in enumerate(moves)
         ]
 
+    def split_copies(lap):
+        west_rows = (pl.ds(1, rows - 4), pl.ds(rows - 3, 4))
+        east_rows = (pl.ds(5, rows - 4), pl.ds(1, 4))
+        north_pairs = (pl.ds(1, pairs - 2), pl.ds(pairs - 1, 2))
+        south_pairs = (pl.ds(3, pairs - 2), pl.ds(1, 2))
+        pieces = []
+        for n in range(2):
+            line = (
+                (lap.at[1, north_pairs[n]], lap.at[rows + 1, north_pairs[n]]),
+                (lap.at[rows, south_pairs[n]], lap.at[0, south_pairs[n]]),
+                (lap.at[west_rows[n], 1, low_half], lap.at[west_rows[n], pairs + 1, low_half]),
+                (lap.at[east_rows[n], pairs, high_half], lap.at[east_rows[n], 0, high_half]),
+            )
+            pieces.append(
+                [
+                    remote(source, target, k, edge_send.at[1 + n, k], edge_recv.at[1 + n, k])
+                    for k, (source, target) in enumerate(line)
+                ]
+            )
+        return pieces
+
     left_tile, right_tile = mpad.at[pl.ds(0, SUB)], mpad.at[pl.ds(wide - SUB, SUB)]
     mass_moves = (
         (mpad, mside.at[1]), (mpad, mside.at[0]),
@@ -265,7 +286,20 @@
         return tiles
 
     def second(e, g):
-        values = [assembled(lap1, e, a, (2 * g, 2 * g + 1)) for a in range(4)]
+        values = []
+        for a in range(4):
+            r = 4 * e + a
+            parts = []
+            for p in range(4):
+                part = lap1[r + 1, 2 * g + p]
+                if a == 0:
+                    part = part + lap1[r, 2 * g + p]
+                if a == 3:
+                    part = part + lap1[r + 2, 2 * g + p]
+                parts.append(part)
+            left_tile = parts[1] + jnp.where(high, 0.0, swap(parts[0]))
+            right_tile = parts[2] + jnp.where(high, swap(parts[3]), 0.0)
+            values.append([left_tile * weights[3, r, 2 * g], right_tile * weights[3, r, 2 * g + 1]])
         keep(lap2, e, g, laplace(values, e, g))
 
     inner_blocks = range(1, blocks_y - 1)
@@ -285,24 +319,35 @@
 
         return body
 
-    loop(1, blocks_x - 1, over(inner_blocks))
-
-    for copy in mass_copies:
-        copy.wait_recv()
+    inner_count = blocks_y - 2
+    loop(0, (blocks_x - 2) * inner_count, lambda i: second(1 + i // inner_count, 1 + i % inner_count))
 
     def with_ends(centre, before, after):
         total = over_columns(centre)
-        total = total + jnp.where(cid == 0, jnp.broadcast_to(before, (wide, LANES)), zero)
-        return total + jnp.where(cid == cols - 1, jnp.broadcast_to(after, (wide, LANES)), zero)
+        if before is not None:
+            total = total + jnp.where(cid == 0, jnp.broadcast_to(before, (wide, LANES)), zero)
+        if after is not None:
+            total = total + jnp.where(cid == cols - 1, jnp.broadcast_to(after, (wide, LANES)), zero)
+        return total
+
+    def whole_inverse(north_east, south_west):
+        own = with_ends(mpad[...], mrow[0, last : last + 1], mrow[1, 0:1])
+        north = with_ends(mside[0], mcorner[0, last : last + 1], north_east)
+        south = with_ends(mside[1], south_west, mcorner[3, 0:1])
+        total = over_rows(own)
+        total = total + jnp.where(rid == 0, pltpu.roll(north, LANES - rows + 1, 1), zero)
+        return inverse(total + jnp.where(rid == rows - 1, pltpu.roll(south, rows - 1, 1), zero))
+
+    def renew(full, r, p):
+        start = 2 * p // SUB * SUB
+        column[3, r, pl.ds(start, SUB), :] = jnp.broadcast_to(full[start : start + SUB, r : r + 1], (SUB, LANES))
+        pair_tile(3, r, p)
 
     last = (cols - 1) % SUB
-    own = with_ends(mpad[...], mrow[0, last : last + 1], mrow[1, 0:1])
-    north = with_ends(mside[0], mcorner[0, last : last + 1], mcorner[1, 0:1])
-    south = with_ends(mside[1], mcorner[2, last : last + 1], mcorner[3, 0:1])
-    total = over_rows(own)
-    total = total + jnp.where(rid == 0, pltpu.roll(north, LANES - rows + 1, 1), zero)
-    total = total + jnp.where(rid == rows - 1, pltpu.roll(south, rows - 1, 1), zero)
-    full = inverse(total)
+    near = (0, 1, 2, 3, 4, 7)
+    for k in near:
+        mass_copies[k].wait_recv()
+    full = whole_inverse(None, None)
     for r in range(rows):
         if r in (0, rows - 1):
             column[3, r] = jnp.broadcast_to(full[:, r : r + 1], (wide, LANES))
@@ -310,23 +355,32 @@
                 pair_tile(3, r, p)
         else:
             for p in (0, pairs - 1):
-                start = 2 * p // SUB * SUB
-                column[3, r, pl.ds(start, SUB), :] = jnp.broadcast_to(full[start : start + SUB, r : r + 1], (SUB, LANES))
-                pair_tile(3, r, p)
-
-    for copy in first_copies:
-        copy.wait_recv()
-
-    second_copies = edge_copies(1, lap2)
-    loop(0, 2, lambda i: over(rim_blocks)(i * (blocks_x - 1)))
-    for copy in second_copies[4:]:
+                renew(full, r, p)
+
+    second_copies = edge_copies(1, lap2)[4:]
+    bulk, tip = split_copies(lap2)
+    for k in near:
+        first_copies[k].wait_recv()
+    loop(0, 2, lambda i: second(i * (blocks_x - 1), i * (blocks_y - 1)))
+    second_copies[0].start()
+    second_copies[3].start()
+    loop(0, 2 * (blocks_x - 2), lambda i: second(1 + i // 2, i % 2 * (blocks_y - 1)))
+    bulk[2].start()
+    bulk[3].start()
+    for k in (5, 6):
+        mass_copies[k].wait_recv()
+    full = whole_inverse(mcorner[1, 0:1], mcorner[2, last : last + 1])
+    renew(full, 0, pairs - 1)
+    renew(full, rows - 1, 0)
+    for k in (5, 6):
+        first_copies[k].wait_recv()
+    loop(0, 2, lambda i: second(i * (blocks_x - 1), (1 - i) * (blocks_y - 1)))
+    for copy in second_copies[1:3] + tip[2:] + tip[:2]:
         copy.start()
-    loop(1, blocks_x - 1, over(rim_blocks))
-    for copy in second_copies[2:4]:
-        copy.start()
-    loop(0, 2, lambda i: over(inner_blocks)(i * (blocks_x - 1)))
-    for copy in second_copies[:2]:
-        copy.start()
+    loop(0, 2 * inner_count, lambda i: second(i // inner_count * (blocks_x - 1), 1 + i % inner_count))
+    bulk[0].start()
+    bulk[1].start()
+    second_copies = second_copies + bulk + tip
 
     def write(e, a, window):
         for p, tile in zip(window, assembled(lap2, e, a, window)):
@@ -388,8 +442,8 @@
                 pltpu.SemaphoreType.DMA((rows // 4 + 3,)),
                 pltpu.SemaphoreType.DMA((8,)),
                 pltpu.SemaphoreType.DMA((8,)),
-                pltpu.SemaphoreType.DMA((2, 8)),
-                pltpu.SemaphoreType.DMA((2, 8)),
+                pltpu.SemaphoreType.DMA((3, 8)),
+                pltpu.SemaphoreType.DMA((3, 8)),
             ],
             compiler_params=pltpu.CompilerParams(collective_id=0, has_side_effects=True),
         )(tiles, metric_diag.transpose(1, 0, 2), metric_cross, point_mass)

time: 37.6 us -> 36.9 us (0.981)
  the two profiles are of different devices: /device:TPU:8 before, /device:TPU:1 now
where the time goes in v4:
time: 36.9 us; the launch traced here: 36.8 us
  Pallas kernels  35.9 us (97%)
  local copies, waits for them, and re-layouts  0.89 us (2%)
    pallas_call x1, Pallas kernels, shards(): pl.pallas_call(functools.partial(operator_kernel, faces, cols_axis, rows,...  35.9 us
    unnamed x1, local copies, waits for them, and re-layouts  0.89 us

profile of v4, /device:TPU:1, one launch (start us, length us, event | category | flops | bytes accessed | tf_op | source)
XLA Modules:
  0.0 36.8 jit_solution(10466422867588745948)
XLA Ops:
  0.0 35.9 %shard_map.46 = f32[20,10,8,128]{3,2,1,0:T(8,128)S(1)} custom-call(f32[20,10,8,128]{3,2,1,0:T(8,128)} %bitcast.8, f32[20,2,20]{2,1,0:T(2,128)} %bitcast.9, f32[20,20]{1,0:T(8,128)} %cross.1, f32[20,20]{1,0:T(8,128)} %mass.1), custom_call_target="tpu_custom_call" | custom-call | tf_op jit(solution)/shard_map/pallas_call | solution.py:424
  35.9 0.9 %copy.6 = f32[4,20,20,128]{3,0,2,1:T(4,128)} copy(f32[4,20,20,128]{3,0,2,1:T(4,128)S(1)} %bitcast.7) | data formatting | bytes 1638400

commit v5 on v4

--- a/solution.py
+++ b/solution.py
@@ -330,11 +330,9 @@
             total = total + jnp.where(cid == cols - 1, jnp.broadcast_to(after, (wide, LANES)), zero)
         return total
 
-    def whole_inverse(north_east, south_west):
-        own = with_ends(mpad[...], mrow[0, last : last + 1], mrow[1, 0:1])
-        north = with_ends(mside[0], mcorner[0, last : last + 1], north_east)
-        south = with_ends(mside[1], south_west, mcorner[3, 0:1])
-        total = over_rows(own)
+    def whole_inverse(west, east, north_west, north_east, south_west, south_east):
+        north, south = with_ends(mside[0], north_west, north_east), with_ends(mside[1], south_west, south_east)
+        total = over_rows(with_ends(mpad[...], west, east))
         total = total + jnp.where(rid == 0, pltpu.roll(north, LANES - rows + 1, 1), zero)
         return inverse(total + jnp.where(rid == rows - 1, pltpu.roll(south, rows - 1, 1), zero))
 
@@ -344,42 +342,56 @@
         pair_tile(3, r, p)
 
     last = (cols - 1) % SUB
-    near = (0, 1, 2, 3, 4, 7)
-    for k in near:
-        mass_copies[k].wait_recv()
-    full = whole_inverse(None, None)
-    for r in range(rows):
-        if r in (0, rows - 1):
-            column[3, r] = jnp.broadcast_to(full[:, r : r + 1], (wide, LANES))
-            for p in range(pairs):
-                pair_tile(3, r, p)
-        else:
-            for p in (0, pairs - 1):
-                renew(full, r, p)
+    def arrive(copies, which):
+        for k in which:
+            copies[k].wait_recv()
 
     second_copies = edge_copies(1, lap2)[4:]
     bulk, tip = split_copies(lap2)
-    for k in near:
-        first_copies[k].wait_recv()
-    loop(0, 2, lambda i: second(i * (blocks_x - 1), i * (blocks_y - 1)))
+
+    arrive(mass_copies, (0, 1))
+    full = whole_inverse(None, None, None, None, None, None)
+    for r in (0, rows - 1):
+        column[3, r] = jnp.broadcast_to(full[:, r : r + 1], (wide, LANES))
+        for p in range(pairs):
+            pair_tile(3, r, p)
+    arrive(first_copies, (0, 1))
+    loop(0, 2 * inner_count, lambda i: second(i // inner_count * (blocks_x - 1), 1 + i % inner_count))
+
+    arrive(mass_copies, (2, 4))
+    from_east = (mrow[1, 0:1], mcorner[3, 0:1])
+    full = whole_inverse(None, from_east[0], None, None, None, from_east[1])
+    for r in range(rows):
+        renew(full, r, pairs - 1)
+    arrive(first_copies, (2, 4))
+    second(blocks_x - 1, blocks_y - 1)
+    second_copies[3].start()
+    loop(1, blocks_x - 1, lambda e: second(e, blocks_y - 1))
+    bulk[3].start()
+    bulk[1].start()
+
+    arrive(mass_copies, (3, 7))
+    from_west = (mrow[0, last : last + 1], mcorner[0, last : last + 1])
+    full = whole_inverse(from_west[0], from_east[0], from_west[1], None, None, from_east[1])
+    for r in range(rows):
+        renew(full, r, 0)
+    arrive(first_copies, (3, 7))
+    second(0, 0)
     second_copies[0].start()
-    second_copies[3].start()
-    loop(0, 2 * (blocks_x - 2), lambda i: second(1 + i // 2, i % 2 * (blocks_y - 1)))
+    loop(1, blocks_x - 1, lambda e: second(e, 0))
     bulk[2].start()
-    bulk[3].start()
-    for k in (5, 6):
-        mass_copies[k].wait_recv()
-    full = whole_inverse(mcorner[1, 0:1], mcorner[2, last : last + 1])
+    bulk[0].start()
+
+    arrive(mass_copies, (5, 6))
+    full = whole_inverse(
+        from_west[0], from_east[0], from_west[1], mcorner[1, 0:1], mcorner[2, last : last + 1], from_east[1]
+    )
     renew(full, 0, pairs - 1)
     renew(full, rows - 1, 0)
-    for k in (5, 6):
-        first_copies[k].wait_recv()
+    arrive(first_copies, (5, 6))
     loop(0, 2, lambda i: second(i * (blocks_x - 1), (1 - i) * (blocks_y - 1)))
     for copy in second_copies[1:3] + tip[2:] + tip[:2]:
         copy.start()
-    loop(0, 2 * inner_count, lambda i: second(i // inner_count * (blocks_x - 1), 1 + i % inner_count))
-    bulk[0].start()
-    bulk[1].start()
     second_copies = second_copies + bulk + tip
 
     def write(e, a, window):

time: 36.9 us -> 36.4 us (0.986)
  the two profiles are of different devices: /device:TPU:1 before, /device:TPU:8 now
where the time goes in v5:
time: 36.4 us; the launch traced here: 36.3 us
  Pallas kernels  35.4 us (97%)
  local copies, waits for them, and re-layouts  0.89 us (2%)
    pallas_call x1, Pallas kernels, shards(): pl.pallas_call(functools.partial(operator_kernel, faces, cols_axis, rows,...  35.4 us
    unnamed x1, local copies, waits for them, and re-layouts  0.89 us

profile of v5, /device:TPU:8, one launch (start us, length us, event | category | flops | bytes accessed | tf_op | source)
XLA Modules:
  0.0 36.3 jit_solution(13952203930489493901)
XLA Ops:
  0.0 35.4 %shard_map.46 = f32[20,10,8,128]{3,2,1,0:T(8,128)S(1)} custom-call(f32[20,10,8,128]{3,2,1,0:T(8,128)} %bitcast.8, f32[20,2,20]{2,1,0:T(2,128)} %bitcast.9, f32[20,20]{1,0:T(8,128)} %cross.1, f32[20,20]{1,0:T(8,128)} %mass.1), custom_call_target="tpu_custom_call" | custom-call | tf_op jit(solution)/shard_map/pallas_call | solution.py:436
  35.4 0.9 %copy.6 = f32[4,20,20,128]{3,0,2,1:T(4,128)} copy(f32[4,20,20,128]{3,0,2,1:T(4,128)S(1)} %bitcast.7) | data formatting | bytes 1638400

commit v6 on v5

--- a/solution.py
+++ b/solution.py
@@ -398,7 +398,7 @@
         for p, tile in zip(window, assembled(lap2, e, a, window)):
             out[4 * e + a, p] = tile
 
-    middle, rim = tuple(range(1, pairs - 1)), (0, pairs - 1)
+    middle = tuple(range(1, pairs - 1))
 
     def write_rows(window):
         for a in range(1, 4):
@@ -413,11 +413,24 @@
         loop(1, blocks_x - 1, body)
 
     write_rows(middle)
-    for copy in second_copies:
+    for copy in bulk[:2] + tip[:2]:
         copy.wait_recv()
-    write_rows(rim)
-    write(0, 0, tuple(range(pairs)))
-    write(blocks_x - 1, 3, tuple(range(pairs)))
+    write(0, 0, middle)
+    write(blocks_x - 1, 3, middle)
+
+    def write_side(p):
+        def body(e):
+            for a in range(4):
+                write(e, a, (p,))
+
+        loop(0, blocks_x, body)
+
+    for copy in (bulk[2], tip[2], second_copies[0], second_copies[2]):
+        copy.wait_recv()
+    write_side(pairs - 1)
+    for copy in (bulk[3], tip[3], second_copies[1], second_copies[3]):
+        copy.wait_recv()
+    write_side(0)
 
     for copy in mass_copies + first_copies + second_copies:
         copy.wait_send()

time: 36.4 us -> 36.4 us (level)
  no operation moved by 1% of the time
where the time goes in v6:
time: 36.4 us; the launch traced here: 36.3 us
  Pallas kernels  35.4 us (97%)
  local copies, waits for them, and re-layouts  0.89 us (2%)
    pallas_call x1, Pallas kernels, shards(): pl.pallas_call(functools.partial(operator_kernel, faces, cols_axis, rows,...  35.4 us
    unnamed x1, local copies, waits for them, and re-layouts  0.89 us

profile of v6, /device:TPU:8, one launch (start us, length us, event | category | flops | bytes accessed | tf_op | source)
XLA Modules:
  0.0 36.3 jit_solution(14133625917687203402)
XLA Ops:
  0.0 35.4 %shard_map.46 = f32[20,10,8,128]{3,2,1,0:T(8,128)S(1)} custom-call(f32[20,10,8,128]{3,2,1,0:T(8,128)} %bitcast.8, f32[20,2,20]{2,1,0:T(2,128)} %bitcast.9, f32[20,20]{1,0:T(8,128)} %cross.1, f32[20,20]{1,0:T(8,128)} %mass.1), custom_call_target="tpu_custom_call" | custom-call | tf_op jit(solution)/shard_map/pallas_call | solution.py:449
  35.4 0.9 %copy.6 = f32[4,20,20,128]{3,0,2,1:T(4,128)} copy(f32[4,20,20,128]{3,0,2,1:T(4,128)S(1)} %bitcast.7) | data formatting | bytes 1638400

commit v7 on v6

--- a/solution.py
+++ b/solution.py
@@ -234,12 +234,12 @@
             )
         return pieces
 
-    left_tile, right_tile = mpad.at[pl.ds(0, SUB)], mpad.at[pl.ds(wide - SUB, SUB)]
+    left_tile, right_tile = mpad.at[low_half], mpad.at[pl.ds(wide - SUB, half)]
     mass_moves = (
         (mpad, mside.at[1]), (mpad, mside.at[0]),
-        (left_tile, mrow.at[1]), (right_tile, mrow.at[0]),
-        (left_tile, mcorner.at[3]), (right_tile, mcorner.at[2]),
-        (left_tile, mcorner.at[1]), (right_tile, mcorner.at[0]),
+        (left_tile, mrow.at[1, low_half]), (right_tile, mrow.at[0, low_half]),
+        (left_tile, mcorner.at[3, low_half]), (right_tile, mcorner.at[2, low_half]),
+        (left_tile, mcorner.at[1, low_half]), (right_tile, mcorner.at[0, low_half]),
     )
     mass_copies = [
         remote(source, target, k, mass_send.at[k], mass_recv.at[k])

time: 36.4 us -> 36.4 us (level)
  no operation moved by 1% of the time
where the time goes in v7:
time: 36.4 us; the launch traced here: 36.2 us
  Pallas kernels  35.3 us (97%)
  local copies, waits for them, and re-layouts  0.89 us (2%)
    pallas_call x1, Pallas kernels, shards(): pl.pallas_call(functools.partial(operator_kernel, faces, cols_axis, rows,...  35.3 us
    unnamed x1, local copies, waits for them, and re-layouts  0.89 us

profile of v7, /device:TPU:8, one launch (start us, length us, event | category | flops | bytes accessed | tf_op | source)
XLA Modules:
  0.0 36.2 jit_solution(6375397677832688948)
XLA Ops:
  0.0 35.3 %shard_map.46 = f32[20,10,8,128]{3,2,1,0:T(8,128)S(1)} custom-call(f32[20,10,8,128]{3,2,1,0:T(8,128)} %bitcast.8, f32[20,2,20]{2,1,0:T(2,128)} %bitcast.9, f32[20,20]{1,0:T(8,128)} %cross.1, f32[20,20]{1,0:T(8,128)} %mass.1), custom_call_target="tpu_custom_call" | custom-call | tf_op jit(solution)/shard_map/pallas_call | solution.py:449
  35.3 0.9 %copy.6 = f32[4,20,20,128]{3,0,2,1:T(4,128)} copy(f32[4,20,20,128]{3,0,2,1:T(4,128)S(1)} %bitcast.7) | data formatting | bytes 1638400
